TPU v7x, 256 devices: a whole 4x4x8 slice. The times are simulated.
256 devices in a mesh: azim: 128 (over x_hi, y, z, core), rad: 2 (over x_lo).
Axes of the slice: x: 4 (x_hi: 2, x_lo: 2; x = x_hi * 2 + x_lo), y: 4, z: 8, core: 2. Of those that a mesh axis runs over, the one named last changes fastest.
Arguments:
- acoustic_state: float32 [5, 1024, 32, 128], P(None, 'azim', 'rad'), may hold values from -6 to 6
- mean_flow: float32 [3, 32, 128], P(None, 'rad'), may hold values from -0.5 to 0.5
- sector_offset: int32 [2], replicated, may hold values from 0 to 127
- cell_shift: int32 [2, 1024], P(None, 'azim'), may hold values from -3 to 0
- stencil_start: int32 [2, 1024], P(None, 'azim'), may hold values from 0 to 1
- interface_fraction: float32 [2, 1024], P(None, 'azim'), may hold values from 0 to 1
Outputs:
- next_state: float32 [5, 1024, 32, 128], P(None, 'azim', 'rad')
All inputs are finite; a program needn't handle non-finite values.
Results may differ from a plain program's by a relative error of at most 0.00005.
Values sent between devices are 32-bit elements; how exact they have to be, the bound alone decides.
A program may use at most 64 MiB of HBM per device.

v0:
```python
import jax
import jax.numpy as jnp
from jax import lax
from jax.experimental import pallas as pl
from jax.experimental.pallas import tpu as pltpu
from jax.sharding import PartitionSpec as P

STENCIL = (0.841570125482, -0.244678631765, 0.059463584768, -0.007650904064)
STEP_SIZE = 0.2
MESH = pl.DeviceIdType.MESH
F32 = jnp.float32

NZ, NY, NX = 8, 4, 2
N = 128


def lanes(rows=8):
    return lax.broadcasted_iota(jnp.int32, (rows, 128), 1)


def moved(value, by):
    return value if by % 128 == 0 else pltpu.roll(value, (-by) % 128, value.ndim - 1)


def forcing(dx, dr, da):
    spread = dx[1] + dr[2] + da[3]
    return [spread, dx[4], dr[4], da[4], spread]


def kernel(offset_ref, shift_ref, start_ref, fraction_ref, flow_hbm, state_hbm, out_hbm,
           E, mid, slot_c0, slot_c1, slot_z0, slot_z1, slot_y0, slot_y1, slot_x0, slot_x1, facing, own_coef, flow, flow_pack,
           own_pack, face_pad, slope, face_mid, own_fix, fix_wide,
           send_sem, recv_sem, fixed_send, fixed_recv, local_sem):
    slots_c, slots_z, slots_y, slots_x = (slot_c0, slot_c1), (slot_z0, slot_z1), (slot_y0, slot_y1), (slot_x0, slot_x1)
    i = lax.axis_index("azim")
    r = lax.axis_index("rad")
    core, z, y, x = i % 2, (i // 2) % NZ, (i // 16) % NY, i // 64
    row0 = pl.multiple_of(8 + 8 * r, 8)
    far0 = pl.multiple_of(8 + 16 * r, 8)
    up, down = (i + 1) % N, (i + N - 1) % N

    def at(azim, rad=None):
        return {"azim": azim, "rad": r if rad is None else rad}

    core_to = i + 1 - 2 * core
    z_to = [i - 2 * z + 2 * ((z + d) % NZ) for d in range(1, NZ)]
    y_to = [i - 16 * y + 16 * ((y + d) % NY) for d in range(1, NY)]
    x_to = (i + 64) % N

    load = pltpu.make_async_copy(state_hbm, E.at[0, :, pl.ds(8, 8), pl.ds(row0, 16), :], local_sem.at[0])
    load.start()
    load_flow = pltpu.make_async_copy(flow_hbm, flow.at[:, pl.ds(pl.multiple_of(8 * r, 8), 16), :], local_sem.at[1])
    load_flow.start()

    barrier = pltpu.get_barrier_semaphore()
    partners = [at(core_to)] + [at(j) for j in z_to] + [at(j) for j in y_to] + [at(x_to)]
    partners += [at(up), at(down), at(i, 1 - r), at(up, 1 - r), at(down, 1 - r)]
    for partner in partners:
        pl.semaphore_signal(barrier, inc=1, device_id=partner, device_id_type=MESH)

    edge = jnp.zeros((5, 16, 8, 128), F32)
    corner = jnp.zeros((5, 4, 8, 128), F32)
    for n in range(2):
        E[n, :, 4:20, 0:8, :] = edge
        E[n, :, 4:20, 32:40, :] = edge
        far_own = pl.multiple_of(24 - 16 * r, 8)
        E[n, :, 0:4, pl.ds(far_own, 8), :] = corner
        E[n, :, 20:24, pl.ds(far_own, 8), :] = corner
    mid[:, :, 0:8, :] = edge
    mid[:, :, 32:40, :] = edge
    face_pad[:, :, 0:8, :] = jnp.zeros((5, 3, 8, 128), F32)
    face_pad[:, :, 32:40, :] = jnp.zeros((5, 3, 8, 128), F32)

    lane = lanes()
    cell_of = lane // 16
    upper = lane % 16 >= 8
    row = lax.broadcasted_iota(jnp.int32, (8, 128), 0)

    def spread_cells(get):
        value = jnp.full((8, 128), get(0))
        for a in range(1, 8):
            value = jnp.where(cell_of == a, get(a), value)
        return value

    def weights(t, m):
        up_one, down_one, down_two = t + 1.0, t - 1.0, t - 2.0
        w = (-t * down_one * down_two / 6.0, up_one * down_one * down_two / 2.0,
             -up_one * t * down_two / 2.0, up_one * t * down_one / 6.0)
        value = jnp.zeros((8, 128), F32)
        for p in range(4):
            value = jnp.where(m == p, w[p], value)
        return value

    stator_t = spread_cells(lambda a: fraction_ref[0, a])
    rotor_t = spread_cells(lambda a: fraction_ref[1, a])
    for n in range(2):
        stator = weights(stator_t, row - spread_cells(lambda a: shift_ref[n, a] + start_ref[0, a] + 3))
        rotor = weights(rotor_t, row - spread_cells(lambda a: start_ref[1, a] - shift_ref[n, a]))
        own_coef[1, n] = jnp.where(upper, stator, rotor)
        slots_c[n][core, 10] = jnp.where(upper, rotor, stator)

    load.wait()
    load_flow.wait()
    pl.semaphore_wait(barrier, len(partners))

    fixed = []

    def send_fixed(src, dst, to):
        no = len(fixed)
        copy = pltpu.make_async_remote_copy(src, dst, fixed_send.at[no], fixed_recv.at[no], device_id=to, device_id_type=MESH)
        copy.start()
        fixed.append(copy)

    send_fixed(own_coef.at[1], own_coef.at[0], at(up))
    send_fixed(own_coef.at[1], own_coef.at[2], at(down))
    send_fixed(flow.at[:, pl.ds(8, 8), :], flow.at[:, pl.ds(pl.multiple_of(16 * r, 8), 8), :], at(i, 1 - r))

    half = lane % 64
    strip = lane % 16
    ahead = [jnp.where(half + j < 64, STENCIL[j - 1], 0.0) for j in range(1, 5)]
    behind = [jnp.where(half - j >= 0, STENCIL[j - 1], 0.0) for j in range(1, 5)]

    def tall(v):
        return jnp.concatenate([v, v, v], axis=0)

    in_ahead = [tall(jnp.where(strip % 8 + j < 8, STENCIL[j - 1], 0.0)) for j in range(1, 5)]
    in_behind = [tall(jnp.where(strip % 8 - j >= 0, STENCIL[j - 1], 0.0)) for j in range(1, 5)]
    cross_ahead = [tall(jnp.where((strip < 8) & (strip + j >= 8), STENCIL[j - 1], 0.0)) for j in range(1, 5)]
    cross_behind = [tall(jnp.where((strip >= 8) & (strip - j < 8), STENCIL[j - 1], 0.0)) for j in range(1, 5)]
    lane24 = lanes(24)

    def taps(value, fore, aft):
        total = None
        for j in range(1, 5):
            term = fore[j - 1] * moved(value, j) - aft[j - 1] * moved(value, -j)
            total = term if total is None else total + term
        return total

    def by_cells(packs, d, outs=(0, 1, 2)):
        if d == 0:
            return [packs[p] for p in outs]
        turned = [moved(v, 16 * d) for v in packs]
        given = []
        for p in outs:
            q = p + (1 if d > 0 else -1)
            if q < 0 or q > 2:
                given.append(turned[p])
            elif d > 0:
                given.append(jnp.where(lane24 < 128 - 16 * d, turned[p], turned[q]))
            else:
                given.append(jnp.where(lane24 >= -16 * d, turned[p], turned[q]))
        return given

    def evaluate_rows(ref, c, t):
        low = 8 + 8 * t
        dx, dr, da, mine = [], [], [], []
        for f in range(5):
            here = ref[f, c, low:low + 8, :]
            mine.append(here)
            dx.append(taps(here, ahead, behind))
            radial = azimuthal = None
            for j in range(1, 5):
                step = STENCIL[j - 1] * (ref[f, c, low + j:low + j + 8, :] - ref[f, c, low - j:low - j + 8, :])
                radial = step if radial is None else radial + step
                step = STENCIL[j - 1] * (ref[f, c + j, low:low + 8, :] - ref[f, c - j, low:low + 8, :])
                azimuthal = step if azimuthal is None else azimuthal + step
            dr.append(radial)
            da.append(azimuthal)
        u = [flow[k, 8 * t:8 * t + 8, :] for k in range(3)]
        push = forcing(dx, dr, da)
        return mine, [-(u[0] * dx[f] + u[1] * dr[f] + u[2] * da[f]) - push[f] for f in range(5)]

    def pack_own(n, t):
        for f in range(5):
            rows = pl.ds(pl.multiple_of(row0 + 8 * t, 8), 8)
            packed = None
            for a in range(8):
                turned = moved(E[n, f, 8 + a, rows, :], 56 - 16 * a)
                packed = turned if packed is None else jnp.where(cell_of == a, turned, packed)
            slots_c[n][core, t * 5 + f] = packed

    def step(n):
        slot_c, slot_z, slot_y, slot_x = slots_c[n], slots_z[n], slots_y[n], slots_x[n]
        k = offset_ref[n]
        source_r = (i - k + N) % N
        source_s = (i + k) % N
        number = [0]
        started = []

        def send(src, dst, to):
            no = number[0]
            number[0] += 1
            copy = pltpu.make_async_remote_copy(src, dst, send_sem.at[n, no], recv_sem.at[n, no], device_id=to, device_id_type=MESH)
            copy.start()
            started.append(copy)
            return copy

        def chosen(slots, digit):
            from_r, from_s = digit(source_r), digit(source_s)
            return jnp.where(upper[None], slots[from_r], slots[from_s])

        pack_own(n, 0)
        pack_own(n, 1)
        mine = slot_c.at[core]
        stage = [send(mine, mine, at(core_to))]
        for copy in stage:
            copy.wait_recv()

        slot_z[z] = chosen(slot_c, lambda s: s % 2)
        mine = slot_z.at[z]
        stage = [send(mine, mine, at(j)) for j in z_to]
        halos = []
        own_rows, far_rows = pl.ds(row0, 16), pl.ds(far0, 8)
        halos.append(send(E.at[n, :, pl.ds(8, 8), own_rows, :], E.at[n, :, pl.ds(0, 8), own_rows, :], at(up)))
        halos.append(send(E.at[n, :, pl.ds(8, 8), own_rows, :], E.at[n, :, pl.ds(16, 8), own_rows, :], at(down)))
        halos.append(send(E.at[n, :, pl.ds(8, 8), pl.ds(16, 8), :], E.at[n, :, pl.ds(8, 8), far_rows, :], at(i, 1 - r)))
        halos.append(send(E.at[n, :, pl.ds(12, 4), pl.ds(16, 8), :], E.at[n, :, pl.ds(4, 4), far_rows, :], at(up, 1 - r)))
        halos.append(send(E.at[n, :, pl.ds(8, 4), pl.ds(16, 8), :], E.at[n, :, pl.ds(16, 4), far_rows, :], at(down, 1 - r)))
        for copy in stage:
            copy.wait_recv()

        slot_y[y] = chosen(slot_z, lambda s: (s // 2) % NZ)
        mine = slot_y.at[y]
        stage = [send(mine, mine, at(j)) for j in y_to]
        for copy in stage:
            copy.wait_recv()

        slot_x[x] = chosen(slot_y, lambda s: (s // 16) % NY)
        mine = slot_x.at[x]
        stage = [send(mine, mine, at(x_to))]
        for copy in halos:
            copy.wait_recv()

        def first(c, carry):
            for t in range(3):
                here, slopes = evaluate_rows(E.at[n], c + 4, t)
                for f in range(5):
                    mid[f, c, 8 + 8 * t:16 + 8 * t, :] = here[f] + (0.5 * STEP_SIZE) * slopes[f]
            return carry

        lax.fori_loop(0, 16, first, 0)

        def strip_of(f, carry):
            for p in range(3):
                packed = None
                for a in range(8):
                    turned = moved(E[n, f, 8 * p + a, 8:32, :], 56 - 16 * a)
                    packed = turned if packed is None else jnp.where(lane24 // 16 == a, turned, packed)
                own_pack[f, p] = packed
            return carry

        lax.fori_loop(0, 5, strip_of, 0)
        for copy in stage:
            copy.wait_recv()

        got = chosen(slot_x, lambda s: s // 64)
        facing[n, 1, pl.ds(5 * r, 10)] = got[0:10]
        facing[n, 1, 15] = got[10]
        rows10, rows5 = pl.ds(5 * r, 10), pl.ds(10 * r, 5)
        stage = []
        for to, place in ((up, 0), (down, 2)):
            stage.append(send(facing.at[n, 1, rows10], facing.at[n, place, rows10], at(to)))
            stage.append(send(facing.at[n, 1, 15], facing.at[n, place, 15], at(to)))
            stage.append(send(facing.at[n, 1, pl.ds(5, 5)], facing.at[n, place, rows5], at(to, 1 - r)))
        stage.append(send(facing.at[n, 1, pl.ds(5, 5)], facing.at[n, 1, rows5], at(i, 1 - r)))
        for copy in stage:
            copy.wait_recv()

        coef_own = [own_coef[p, n] for p in range(3)]
        coef_face = []
        for p in range(3):
            sent = facing[n, p, 15]
            coef_face.append(jnp.where(upper, moved(sent, -8), moved(sent, 8)))

        def strip_slopes(f, carry):
            F = [jnp.concatenate([facing[n, p, 5 * t + f] for t in range(3)], axis=0) for p in range(3)]
            M = [own_pack[f, p] for p in range(3)]
            for p in range(3):
                face_pad[f, p, 8:32, :] = F[p]
            ghost_own = [jnp.zeros((24, 128), F32)] * 3
            ghost_face = [jnp.zeros((24, 128), F32)] * 3
            azimuthal = [jnp.zeros((24, 128), F32)] * 3
            for d in range(-4, 5):
                shifted = by_cells(F, d)
                if d < 4:
                    shifted_own = by_cells(M, d)
                for p in range(3):
                    if d != 0:
                        weight = STENCIL[d - 1] if d > 0 else -STENCIL[-d - 1]
                        azimuthal[p] = azimuthal[p] + weight * shifted[p]
                    if d < 4:
                        ghost_own[p] = ghost_own[p] + coef_own[p][d + 4:d + 5, :] * shifted[p]
                        ghost_face[p] = ghost_face[p] + coef_face[p][d + 4:d + 5, :] * shifted_own[p]
            for p in range(3):
                slope[0, f, p] = taps(F[p], in_ahead, in_behind) + taps(ghost_face[p], cross_ahead, cross_behind)
                radial = None
                for j in range(1, 5):
                    part = STENCIL[j - 1] * (face_pad[f, p, 8 + j:32 + j, :] - face_pad[f, p, 8 - j:32 - j, :])
                    radial = part if radial is None else radial + part
                slope[1, f, p] = radial
                slope[2, f, p] = azimuthal[p]
                own_fix[f, p] = taps(ghost_own[p], cross_ahead, cross_behind)
            return carry

        lax.fori_loop(0, 5, strip_slopes, 0)

        def fixed_by(ux, cut, scale):
            push = [cut[1], cut[4], None, None, cut[1]]
            return [-scale * (ux * cut[f] + push[f]) if push[f] is not None else -scale * (ux * cut[f]) for f in range(5)]

        for p in range(3):
            u = [flow_pack[m] for m in range(3)]
            dx, dr, da = ([slope[m, f, p] for f in range(5)] for m in range(3))
            push = forcing(dx, dr, da)
            for f in range(5):
                change = -(u[0] * dx[f] + u[1] * dr[f] + u[2] * da[f]) - push[f]
                face_mid[f, p] = face_pad[f, p, 8:32, :] + (0.5 * STEP_SIZE) * change
            fix = fixed_by(u[0], [own_fix[f, p] for f in range(5)], 0.5 * STEP_SIZE)
            for f in range(5):
                own_fix[f, p] = fix[f]

        near = (lane24 >= 60) & (lane24 < 68)

        def fix_mid(f, carry):
            for c in range(16):
                p, a = (c + 4) // 8, (c + 4) % 8
                wide = moved(own_fix[f, p], 16 * a - 56)
                mid[f, c, 8:32, :] = mid[f, c, 8:32, :] + jnp.where(near, wide, 0.0)
            ghosts = jnp.zeros((24, 128), F32)
            packs = [face_mid[f, p] for p in range(3)]
            for d in range(-4, 4):
                ghosts = ghosts + coef_own[1][d + 4:d + 5, :] * by_cells(packs, d, (1,))[0]
            slope[0, f, 0] = taps(ghosts, cross_ahead, cross_behind)
            return carry

        lax.fori_loop(0, 5, fix_mid, 0)
        fix = fixed_by(flow_pack[0], [slope[0, f, 0] for f in range(5)], STEP_SIZE)
        for f in range(5):
            slope[1, f, 0] = fix[f]

        def widen(f, carry):
            for a in range(8):
                fix_wide[f, a] = jnp.where(near, moved(slope[1, f, 0], 16 * a - 56), 0.0)
            return carry

        lax.fori_loop(0, 5, widen, 0)

        def second(c, carry):
            after = []
            for t in range(3):
                _, slopes = evaluate_rows(mid, c + 4, t)
                after.append([E[n, f, c + 8, 8 + 8 * t:16 + 8 * t, :] + STEP_SIZE * slopes[f]
                              + fix_wide[f, c, 8 * t:8 * t + 8, :] for f in range(5)])
            for t in range(2):
                for f in range(5):
                    own = jnp.where(r == 0, after[t][f], after[t + 1][f])
                    E[n + 1, f, c + 8, pl.ds(pl.multiple_of(row0 + 8 * t, 8), 8), :] = own
            return carry

        lax.fori_loop(0, 8, second, 0)
        for copy in started:
            copy.wait_send()

    for copy in fixed:
        copy.wait()
    for m in range(3):
        packed = None
        for a in range(8):
            turned = moved(flow[m], 56 - 16 * a)
            packed = turned if packed is None else jnp.where(lane24 // 16 == a, turned, packed)
        flow_pack[m] = packed

    step(0)
    step(1)
    store = pltpu.make_async_copy(E.at[2, :, pl.ds(8, 8), pl.ds(row0, 16), :], out_hbm, local_sem.at[0])
    store.start()
    store.wait()


def shards(acoustic_state, mean_flow, sector_offset, cell_shift, stencil_start, interface_fraction):
    smem = pl.BlockSpec(memory_space=pltpu.SMEM)
    anywhere = pl.BlockSpec(memory_space=pl.ANY)
    vmem = lambda *shape: pltpu.VMEM(shape, F32)
    return pl.pallas_call(
        kernel,
        out_shape=jax.ShapeDtypeStruct(acoustic_state.shape, F32),
        in_specs=[smem, smem, smem, smem, anywhere, anywhere],
        out_specs=anywhere,
        scratch_shapes=[
            vmem(3, 5, 24, 40, 128),
            vmem(5, 16, 40, 128),
            *[vmem(count, 11, 8, 128) for count in (2, NZ, NY, NX) for _ in range(2)],
            vmem(2, 3, 16, 8, 128),
            vmem(3, 2, 8, 128),
            vmem(3, 24, 128),
            vmem(3, 24, 128),
            vmem(5, 3, 24, 128),
            vmem(5, 3, 40, 128),
            vmem(3, 5, 3, 24, 128),
            vmem(5, 3, 24, 128),
            vmem(5, 3, 24, 128),
            vmem(5, 8, 24, 128),
            pltpu.SemaphoreType.DMA((2, 24)),
            pltpu.SemaphoreType.DMA((2, 24)),
            pltpu.SemaphoreType.DMA((3,)),
            pltpu.SemaphoreType.DMA((3,)),
            pltpu.SemaphoreType.DMA((2,)),
        ],
        compiler_params=pltpu.CompilerParams(collective_id=0, has_side_effects=True, vmem_limit_bytes=40 * 1024 * 1024),
        name="acoustic_steps",
    )(sector_offset, cell_shift, stencil_start, interface_fraction, mean_flow, acoustic_state)


def solution(mesh):
    return jax.shard_map(
        shards,
        mesh=mesh,
        in_specs=(
            P(None, "azim", "rad", None),
            P(None, "rad", None),
            P(),
            P(None, "azim"),
            P(None, "azim"),
            P(None, "azim"),
        ),
        out_specs=P(None, "azim", "rad", None),
        check_vma=False,
    )
```

profile of v0, /device:TPU:1, one launch (start us, length us, event | category | flops | bytes accessed | tf_op | source)
XLA Modules:
  0.0 85.5 jit_solution(9239859348444258479)
XLA Ops:
  0.0 0.0 copy-start
  0.0 1.0 %copy-done = f32[5,8,16,128]{3,2,1,0:T(8,128)S(1)} copy-done((f32[5,8,16,128]{3,2,1,0:T(8,128)S(1)}, f32[5,8,16,128]{3,2,1,0:T(8,128)}, u32[]{:S(2)}) %copy-start) | copy-done | bytes 327704
  1.0 0.0 copy-start.1
  1.0 0.7 copy-done.1
  1.7 0.0 copy-start.2
  1.7 0.7 copy-done.2
  2.4 0.0 copy-start.3
  2.4 0.7 copy-done.3
  3.1 0.0 copy-start.4
  3.1 0.7 copy-done.4
  3.8 0.0 copy-start.5
  3.8 0.7 copy-done.5
  4.4 80.4 %acoustic_steps.1 = f32[5,8,16,128]{3,2,1,0:T(8,128)S(1)} custom-call(s32[2]{0:T(128)S(1)} %copy-done.5, s32[2,8]{1,0:T(2,128)S(1)} %copy-done.2, s32[2,8]{1,0:T(2,128)S(1)} %copy-done.3, f32[2,8]{1,0:T(2,128)S(1)} %copy-done.4, f32[3,16,128]{2,1,0:T(8,128)S(1)} %copy-done.1, f32[5,8,16,128]{3,2,1,0:T(8,128)S(1)} %copy-done), custom_call_target="tpu_custom_call" | custom-call | tf_op jit(solution)/shard_map/acoustic_steps/pallas_call | solution.py:384
  84.8 0.7 copy.8
Async XLA Ops:
  0.0 1.0 %copy-start = (f32[5,8,16,128]{3,2,1,0:T(8,128)S(1)}, f32[5,8,16,128]{3,2,1,0:T(8,128)}, u32[]{:S(2)}) copy-start(f32[5,8,16,128]{3,2,1,0:T(8,128)} %state_hbm.1) | copy-start | bytes 983044
  1.0 0.7 copy-start.1
  1.7 0.7 copy-start.2
  2.4 0.7 copy-start.3
  3.1 0.7 copy-start.4
  3.8 0.7 copy-start.5
where the time goes:
time: 85.7 us; the launch traced here: 85.5 us
  Pallas kernels  80.4 us (94%)
  local copies, waits for them, and re-layouts  5.13 us (6%)
    pallas_call x1, Pallas kernels, shards(): pl.pallas_call(kernel, out_shape=jax.ShapeDtypeStruct(acoustic_state.shap...  80.4 us
    unnamed x13, local copies, waits for them, and re-layouts  5.13 us

commit v1 on v0

v1 whole, which is shorter than its diff:
```python
import jax
import jax.numpy as jnp
from jax import lax
from jax.experimental import pallas as pl
from jax.experimental.pallas import tpu as pltpu
from jax.sharding import PartitionSpec as P

STENCIL = (0.841570125482, -0.244678631765, 0.059463584768, -0.007650904064)
STEP_SIZE = 0.2
MESH = pl.DeviceIdType.MESH
F32 = jnp.float32

NZ, NY, NX = 8, 4, 2
N = 128


def lanes(rows=8):
    return lax.broadcasted_iota(jnp.int32, (rows, 128), 1)


def moved(value, by):
    return value if by % 128 == 0 else pltpu.roll(value, (-by) % 128, value.ndim - 1)


def forcing(dx, dr, da):
    spread = dx[1] + dr[2] + da[3]
    return [spread, dx[4], dr[4], da[4], spread]


def kernel(offset_hbm, shift_hbm, start_hbm, fraction_hbm, flow_hbm, state_hbm, out_hbm,
           offset_ref, shift_ref, start_ref, fraction_ref,
           E, mid, slot_a0, slot_a1, slot_z0, slot_z1, slot_y0, slot_y1, slot_x0, slot_x1, facing, own_coef, flow, flow_pack,
           own_pack, face_pad, slope, face_mid, own_fix, next_pack, fix_pad,
           send_sem, recv_sem, fixed_send, fixed_recv, local_sem):
    slots_a, slots_z, slots_y, slots_x = (slot_a0, slot_a1), (slot_z0, slot_z1), (slot_y0, slot_y1), (slot_x0, slot_x1)
    i = lax.axis_index("azim")
    r = lax.axis_index("rad")
    core, z, y, x = i % 2, (i // 2) % NZ, (i // 16) % NY, i // 64
    row0 = pl.multiple_of(8 + 8 * r, 8)
    far0 = pl.multiple_of(8 + 16 * r, 8)
    up, down = (i + 1) % N, (i + N - 1) % N

    def at(azim, rad=None):
        return {"azim": azim, "rad": r if rad is None else rad}

    def along_z(d):
        return i - 2 * z + 2 * ((z + d + NZ) % NZ)

    other = 1 - 2 * core
    near_to = [(i + other, 2 + core)]
    for d in (1, -1):
        near_to += [(along_z(d), 2 * (1 - d) + core), (along_z(d) + other, 2 * (1 - d) + core)]
    z_to = [(along_z(3), 0), (along_z(-3), 2)]
    y_to = [i - 16 * y + 16 * ((y + d) % NY) for d in (2, 1, 3)]
    x_to = (i + 64) % N

    loads = []

    def load(src, dst):
        copy = pltpu.make_async_copy(src, dst, local_sem.at[len(loads)])
        copy.start()
        loads.append(copy)

    load(state_hbm, E.at[0, :, pl.ds(8, 8), pl.ds(row0, 16), :])
    load(flow_hbm, flow.at[:, pl.ds(pl.multiple_of(8 * r, 8), 16), :])
    load(shift_hbm, shift_ref)
    load(start_hbm, start_ref)
    load(fraction_hbm, fraction_ref)
    load(offset_hbm, offset_ref)

    barrier = pltpu.get_barrier_semaphore()
    partners = [at(j) for j, _ in near_to] + [at(j) for j, _ in z_to] + [at(j) for j in y_to] + [at(x_to)]
    partners += [at(up), at(down), at(i, 1 - r), at(up, 1 - r), at(down, 1 - r)]
    for partner in partners:
        pl.semaphore_signal(barrier, inc=1, device_id=partner, device_id_type=MESH)

    edge = jnp.zeros((5, 16, 8, 128), F32)
    corner = jnp.zeros((5, 4, 8, 128), F32)
    for n in range(2):
        E[n, :, 4:20, 0:8, :] = edge
        E[n, :, 4:20, 32:40, :] = edge
        far_own = pl.multiple_of(24 - 16 * r, 8)
        E[n, :, 0:4, pl.ds(far_own, 8), :] = corner
        E[n, :, 20:24, pl.ds(far_own, 8), :] = corner
    for low in (0, 32):
        mid[:, :, low:low + 8, :] = edge
        face_pad[:, :, low:low + 8, :] = jnp.zeros((5, 2, 8, 128), F32)
        fix_pad[:, low:low + 8, :] = jnp.zeros((5, 8, 128), F32)

    lane = lanes()
    cell_of = lane // 16
    upper = lane % 16 >= 8
    row = lax.broadcasted_iota(jnp.int32, (8, 128), 0)

    def spread_cells(get):
        value = jnp.full((8, 128), get(0))
        for a in range(1, 8):
            value = jnp.where(cell_of == a, get(a), value)
        return value

    def weights(t, m):
        up_one, down_one, down_two = t + 1.0, t - 1.0, t - 2.0
        w = (-t * down_one * down_two / 6.0, up_one * down_one * down_two / 2.0,
             -up_one * t * down_two / 2.0, up_one * t * down_one / 6.0)
        value = jnp.zeros((8, 128), F32)
        for p in range(4):
            value = jnp.where(m == p, w[p], value)
        return value

    def pack_rows(n, t, f):
        rows = pl.ds(pl.multiple_of(row0 + 8 * t, 8), 8)
        packed = None
        for a in range(8):
            turned = moved(E[n, f, 8 + a, rows, :], 56 - 16 * a)
            packed = turned if packed is None else jnp.where(cell_of == a, turned, packed)
        return packed

    for copy in loads:
        copy.wait()
    for t in range(2):
        for f in range(5):
            slots_a[0][2 + core, t * 5 + f] = pack_rows(0, t, f)
    stator_t = spread_cells(lambda a: fraction_ref[0, a])
    rotor_t = spread_cells(lambda a: fraction_ref[1, a])
    for n in range(2):
        stator = weights(stator_t, row - spread_cells(lambda a: shift_ref[n, a] + start_ref[0, a] + 3))
        rotor = weights(rotor_t, row - spread_cells(lambda a: start_ref[1, a] - shift_ref[n, a]))
        own_coef[1, n] = jnp.where(upper, stator, rotor)
        slots_a[n][2 + core, 10] = jnp.where(upper, rotor, stator)

    pl.semaphore_wait(barrier, len(partners))
    fixed = []

    def send_fixed(src, dst, to):
        no = len(fixed)
        copy = pltpu.make_async_remote_copy(src, dst, fixed_send.at[no], fixed_recv.at[no], device_id=to, device_id_type=MESH)
        copy.start()
        fixed.append(copy)

    half = lane % 64
    strip = lane % 16
    ahead = [jnp.where(half + j < 64, STENCIL[j - 1], 0.0) for j in range(1, 5)]
    behind = [jnp.where(half - j >= 0, STENCIL[j - 1], 0.0) for j in range(1, 5)]

    def tall(v):
        return jnp.concatenate([v, v, v], axis=0)

    in_ahead = [tall(jnp.where(strip % 8 + j < 8, STENCIL[j - 1], 0.0)) for j in range(1, 5)]
    in_behind = [tall(jnp.where(strip % 8 - j >= 0, STENCIL[j - 1], 0.0)) for j in range(1, 5)]
    cross_ahead = [tall(jnp.where((strip < 8) & (strip + j >= 8), STENCIL[j - 1], 0.0)) for j in range(1, 5)]
    cross_behind = [tall(jnp.where((strip >= 8) & (strip - j < 8), STENCIL[j - 1], 0.0)) for j in range(1, 5)]
    lane24 = lanes(24)

    def taps(value, fore, aft):
        total = None
        for j in range(1, 5):
            term = fore[j - 1] * moved(value, j) - aft[j - 1] * moved(value, -j)
            total = term if total is None else total + term
        return total

    def ring(sectors):
        turned = [moved(v, 64) for v in sectors]
        low = lanes(turned[0].shape[0]) < 64
        return [jnp.where(low, turned[p], turned[(p + 1) % 3]) for p in range(3)]

    def by_cells(packs, d):
        if d == 0:
            return packs[:2]
        turned = [moved(v, 16 * d) for v in packs]
        if d > 0:
            return [jnp.where(lane24 < 128 - 16 * d, turned[p], turned[p + 1]) for p in range(2)]
        return [jnp.where(lane24 >= -16 * d, turned[p], turned[(p + 2) % 3]) for p in range(2)]

    def between(packs, o):
        if o % 8 == 0:
            return packs[o // 8]
        return jnp.where(lane24 < 128 - 16 * o, moved(packs[0], 16 * o), moved(packs[1], 16 * o))

    def evaluate_rows(ref, c, t):
        low = 8 + 8 * t
        dx, dr, da, mine = [], [], [], []
        for f in range(5):
            here = ref[f, c, low:low + 8, :]
            mine.append(here)
            dx.append(taps(here, ahead, behind))
            radial = azimuthal = None
            for j in range(1, 5):
                step = STENCIL[j - 1] * (ref[f, c, low + j:low + j + 8, :] - ref[f, c, low - j:low - j + 8, :])
                radial = step if radial is None else radial + step
                step = STENCIL[j - 1] * (ref[f, c + j, low:low + 8, :] - ref[f, c - j, low:low + 8, :])
                azimuthal = step if azimuthal is None else azimuthal + step
            dr.append(radial)
            da.append(azimuthal)
        u = [flow[k, 8 * t:8 * t + 8, :] for k in range(3)]
        push = forcing(dx, dr, da)
        return mine, [-(u[0] * dx[f] + u[1] * dr[f] + u[2] * da[f]) - push[f] for f in range(5)]

    def radial_of(ref, *index):
        total = None
        for j in range(1, 5):
            part = STENCIL[j - 1] * (ref[(*index, slice(8 + j, 32 + j))] - ref[(*index, slice(8 - j, 32 - j))])
            total = part if total is None else total + part
        return total

    def own_rows_of(value, t):
        return jnp.where(r == 0, value[8 * t:8 * t + 8], value[8 * t + 8:8 * t + 16])

    def step(n):
        slot_a, slot_z, slot_y, slot_x = slots_a[n], slots_z[n], slots_y[n], slots_x[n]
        k = offset_ref[n]
        source_r = (i - k + N) % N
        source_s = (i + k) % N
        low_r = (core - k % 16 + 16) % 16
        low_s = (core + k % 16) % 16
        started = []

        def parts(low):
            far = ((low // 2 + 3) % 8 + 1) // 3 - 1
            near = (low // 2 + 3) % 8 - 3 - 3 * far
            return near, far

        def send(src, dst, to):
            no = len(started)
            copy = pltpu.make_async_remote_copy(src, dst, send_sem.at[n, no], recv_sem.at[n, no], device_id=to, device_id_type=MESH)
            copy.start()
            started.append(copy)
            return copy

        def chosen(slots, from_r, from_s):
            return jnp.where(upper[None], slots[from_r], slots[from_s])

        mine = slot_a.at[2 + core]
        stage = [send(mine, slot_a.at[place], at(j)) for j, place in near_to]

        if n == 0:
            send_fixed(own_coef.at[1], own_coef.at[0], at(up))
            send_fixed(own_coef.at[1], own_coef.at[2], at(down))
            send_fixed(flow.at[:, pl.ds(8, 8), :], flow.at[:, pl.ds(pl.multiple_of(16 * r, 8), 8), :], at(i, 1 - r))
        else:
            def into_rows(f, carry):
                for t in range(2):
                    change = own_rows_of(own_fix[f, 0], t)
                    rows = pl.ds(pl.multiple_of(row0 + 8 * t, 8), 8)
                    for a in range(8):
                        E[1, f, 8 + a, rows, :] = E[1, f, 8 + a, rows, :] + jnp.where(
                            (lane >= 56) & (lane < 72), moved(change, 16 * a - 56), 0.0)
                return carry

            lax.fori_loop(0, 5, into_rows, 0)

        own_rows, far_rows = pl.ds(row0, 16), pl.ds(far0, 8)
        halos = []
        halos.append(send(E.at[n, :, pl.ds(8, 8), pl.ds(16, 8), :], E.at[n, :, pl.ds(8, 8), far_rows, :], at(i, 1 - r)))
        halos.append(send(E.at[n, :, pl.ds(12, 4), pl.ds(16, 8), :], E.at[n, :, pl.ds(4, 4), far_rows, :], at(up, 1 - r)))
        halos.append(send(E.at[n, :, pl.ds(8, 4), pl.ds(16, 8), :], E.at[n, :, pl.ds(16, 4), far_rows, :], at(down, 1 - r)))
        for copy in stage:
            copy.wait_recv()

        (near_r, far_r), (near_s, far_s) = parts(low_r), parts(low_s)
        slot_z[1] = chosen(slot_a, 2 * (near_r + 1) + low_r % 2, 2 * (near_s + 1) + low_s % 2)
        mine = slot_z.at[1]
        stage = [send(mine, slot_z.at[place], at(j)) for j, place in z_to]
        halos.append(send(E.at[n, :, pl.ds(8, 8), own_rows, :], E.at[n, :, pl.ds(0, 8), own_rows, :], at(up)))
        halos.append(send(E.at[n, :, pl.ds(8, 8), own_rows, :], E.at[n, :, pl.ds(16, 8), own_rows, :], at(down)))
        for copy in stage:
            copy.wait_recv()

        slot_y[y] = chosen(slot_z, far_r + 1, far_s + 1)
        mine = slot_y.at[y]
        stage = [send(mine, mine, at(j)) for j in y_to]
        for copy in stage:
            copy.wait_recv()

        slot_x[x] = chosen(slot_y, (source_r // 16) % NY, (source_s // 16) % NY)
        mine = slot_x.at[x]
        stage = [send(mine, mine, at(x_to))]

        if n == 0:
            for copy in fixed:
                copy.wait()
            for m in range(3):
                packed = None
                for a in range(8):
                    turned = moved(flow[m], 56 - 16 * a)
                    packed = turned if packed is None else jnp.where(lane24 // 16 == a, turned, packed)
                flow_pack[m] = packed
        for copy in halos:
            copy.wait_recv()

        def first(c, carry):
            for t in range(3):
                here, slopes = evaluate_rows(E.at[n], c + 4, t)
                for f in range(5):
                    mid[f, c, 8 + 8 * t:16 + 8 * t, :] = here[f] + (0.5 * STEP_SIZE) * slopes[f]
            return carry

        lax.fori_loop(0, 16, first, 0)
        for copy in stage:
            copy.wait_recv()

        got = chosen(slot_x, source_r // 64, source_s // 64)
        facing[n, 1, pl.ds(5 * r, 10)] = got[0:10]
        facing[n, 1, 15] = got[10]
        rows10, rows5 = pl.ds(5 * r, 10), pl.ds(10 * r, 5)
        stage = []
        for to, place in ((up, 0), (down, 2)):
            stage.append(send(facing.at[n, 1, rows10], facing.at[n, place, rows10], at(to)))
            stage.append(send(facing.at[n, 1, 15], facing.at[n, place, 15], at(to)))
            stage.append(send(facing.at[n, 1, pl.ds(5, 5)], facing.at[n, place, rows5], at(to, 1 - r)))
        stage.append(send(facing.at[n, 1, pl.ds(5, 5)], facing.at[n, 1, rows5], at(i, 1 - r)))

        def second(c, carry):
            after = []
            for t in range(3):
                _, slopes = evaluate_rows(mid, c + 4, t)
                after.append([E[n, f, c + 8, 8 + 8 * t:16 + 8 * t, :] + STEP_SIZE * slopes[f] for f in range(5)])
            for t in range(2):
                for f in range(5):
                    own = jnp.where(r == 0, after[t][f], after[t + 1][f])
                    E[n + 1, f, c + 8, pl.ds(pl.multiple_of(row0 + 8 * t, 8), 8), :] = own
            return carry

        lax.fori_loop(0, 8, second, 0)

        def strip_of(f, carry):
            for p in range(3):
                packed = None
                for a in range(8):
                    turned = moved(E[n, f, (4 + 8 * p + a) % 24, 8:32, :], 56 - 16 * a)
                    packed = turned if packed is None else jnp.where(lane24 // 16 == a, turned, packed)
                own_pack[f, p] = packed
            if n == 0:
                for t in range(2):
                    next_pack[t, f] = pack_rows(1, t, f)
            return carry

        lax.fori_loop(0, 5, strip_of, 0)
        coef_own = ring([own_coef[p, n] for p in range(3)])
        for copy in stage:
            copy.wait_recv()

        coef_face = ring([jnp.where(upper, moved(facing[n, p, 15], -8), moved(facing[n, p, 15], 8)) for p in range(3)])

        def strip_slopes(f, carry):
            F = ring([jnp.concatenate([facing[n, p, 5 * t + f] for t in range(3)], axis=0) for p in range(3)])
            M = [own_pack[f, p] for p in range(3)]
            for p in range(2):
                face_pad[f, p, 8:32, :] = F[p]
            ghost_own = [jnp.zeros((24, 128), F32)] * 2
            ghost_face = [jnp.zeros((24, 128), F32)] * 2
            azimuthal = [jnp.zeros((24, 128), F32)] * 2
            for d in range(-4, 5):
                shifted = by_cells(F, d)
                if d < 4:
                    shifted_own = by_cells(M, d)
                for p in range(2):
                    if d != 0:
                        weight = STENCIL[d - 1] if d > 0 else -STENCIL[-d - 1]
                        azimuthal[p] = azimuthal[p] + weight * shifted[p]
                    if d < 4:
                        ghost_own[p] = ghost_own[p] + coef_own[p][d + 4:d + 5, :] * shifted[p]
                        ghost_face[p] = ghost_face[p] + coef_face[p][d + 4:d + 5, :] * shifted_own[p]
            for p in range(2):
                slope[0, f, p] = taps(F[p], in_ahead, in_behind) + taps(ghost_face[p], cross_ahead, cross_behind)
                slope[1, f, p] = radial_of(face_pad, f, p)
                slope[2, f, p] = azimuthal[p]
                own_fix[f, p] = taps(ghost_own[p], cross_ahead, cross_behind)
            return carry

        lax.fori_loop(0, 5, strip_slopes, 0)

        u = [flow_pack[m] for m in range(3)]
        for p in range(2):
            dx, dr, da = ([slope[m, f, p] for f in range(5)] for m in range(3))
            push = forcing(dx, dr, da)
            for f in range(5):
                change = -(u[0] * dx[f] + u[1] * dr[f] + u[2] * da[f]) - push[f]
                face_mid[f, p] = face_pad[f, p, 8:32, :] + (0.5 * STEP_SIZE) * change
            cut = [own_fix[f, p] for f in range(5)]
            push = [cut[1], cut[4], 0.0, 0.0, cut[1]]
            for f in range(5):
                own_fix[f, p] = (-0.5 * STEP_SIZE) * (u[0] * cut[f] + push[f])

        def fix_slopes(f, carry):
            face = [face_mid[f, p] for p in range(2)]
            fix = [own_fix[f, p] for p in range(2)]
            ghosts = jnp.zeros((24, 128), F32)
            azimuthal = jnp.zeros((24, 128), F32)
            for o in range(9):
                if o < 8:
                    ghosts = ghosts + own_coef[1, n, o:o + 1, :] * between(face, o)
                if o != 4:
                    weight = STENCIL[o - 5] if o > 4 else -STENCIL[3 - o]
                    azimuthal = azimuthal + weight * between(fix, o)
            here = between(fix, 4)
            fix_pad[f, 8:32, :] = here
            slope[0, f, 0] = taps(here, in_ahead, in_behind) + taps(ghosts, cross_ahead, cross_behind)
            slope[1, f, 0] = radial_of(fix_pad, f)
            slope[2, f, 0] = azimuthal
            return carry

        lax.fori_loop(0, 5, fix_slopes, 0)
        dx, dr, da = ([slope[m, f, 0] for f in range(5)] for m in range(3))
        push = forcing(dx, dr, da)
        for f in range(5):
            change = -STEP_SIZE * (u[0] * dx[f] + u[1] * dr[f] + u[2] * da[f] + push[f])
            own_fix[f, 0] = change
            if n == 0:
                for t in range(2):
                    slots_a[1][2 + core, 5 * t + f] = next_pack[t, f] + own_rows_of(change, t)
        return started

    started = step(0)
    started += step(1)

    def into_result(f, carry):
        for t in range(2):
            change = own_rows_of(own_fix[f, 0], t)
            rows = pl.ds(pl.multiple_of(row0 + 8 * t, 8), 8)
            for a in range(8):
                E[2, f, 8 + a, rows, :] = E[2, f, 8 + a, rows, :] + jnp.where(
                    (lane >= 56) & (lane < 72), moved(change, 16 * a - 56), 0.0)
        return carry

    lax.fori_loop(0, 5, into_result, 0)
    store = pltpu.make_async_copy(E.at[2, :, pl.ds(8, 8), pl.ds(row0, 16), :], out_hbm, local_sem.at[0])
    store.start()
    for copy in started:
        copy.wait_send()
    store.wait()


def shards(acoustic_state, mean_flow, sector_offset, cell_shift, stencil_start, interface_fraction):
    anywhere = pl.BlockSpec(memory_space=pl.ANY)
    vmem = lambda *shape: pltpu.VMEM(shape, F32)
    smem = lambda value: pltpu.SMEM(value.shape, value.dtype)
    return pl.pallas_call(
        kernel,
        out_shape=jax.ShapeDtypeStruct(acoustic_state.shape, F32),
        in_specs=[anywhere] * 6,
        out_specs=anywhere,
        scratch_shapes=[
            smem(sector_offset),
            smem(cell_shift),
            smem(stencil_start),
            smem(interface_fraction),
            vmem(3, 5, 24, 40, 128),
            vmem(5, 16, 40, 128),
            *[vmem(count, 11, 8, 128) for count in (6, 3, NY, NX) for _ in range(2)],
            vmem(2, 3, 16, 8, 128),
            vmem(3, 2, 8, 128),
            vmem(3, 24, 128),
            vmem(3, 24, 128),
            vmem(5, 3, 24, 128),
            vmem(5, 2, 40, 128),
            vmem(3, 5, 2, 24, 128),
            vmem(5, 2, 24, 128),
            vmem(5, 2, 24, 128),
            vmem(2, 5, 8, 128),
            vmem(5, 40, 128),
            pltpu.SemaphoreType.DMA((2, 24)),
            pltpu.SemaphoreType.DMA((2, 24)),
            pltpu.SemaphoreType.DMA((3,)),
            pltpu.SemaphoreType.DMA((3,)),
            pltpu.SemaphoreType.DMA((6,)),
        ],
        compiler_params=pltpu.CompilerParams(collective_id=0, has_side_effects=True, vmem_limit_bytes=67043328),
        name="acoustic_steps",
    )(sector_offset, cell_shift, stencil_start, interface_fraction, mean_flow, acoustic_state)


def solution(mesh):
    return jax.shard_map(
        shards,
        mesh=mesh,
        in_specs=(
            P(None, "azim", "rad", None),
            P(None, "rad", None),
            P(),
            P(None, "azim"),
            P(None, "azim"),
            P(None, "azim"),
        ),
        out_specs=P(None, "azim", "rad", None),
        check_vma=False,
    )
```

time: 85.7 us -> 68.2 us (0.80)
  Pallas kernels: 80.4 us -> 66 us
  local copies, waits for them, and re-layouts: 5.13 us -> 1.72 us
    pallas_call x1, Pallas kernels: 80.4 us -> 66 us  [shards(): pl.pallas_call(kernel, out_shape=jax.ShapeDtypeStruct(acoustic_state.shap...]
    unnamed x13 -> x1, local copies, waits for them, and re-layouts: 5.13 us -> 1.72 us
where the time goes in v1:
time: 68.2 us; the launch traced here: 67.8 us
  Pallas kernels  66 us (97%)
  local copies, waits for them, and re-layouts  1.72 us (3%)
    pallas_call x1, Pallas kernels, shards(): pl.pallas_call(kernel, out_shape=jax.ShapeDtypeStruct(acoustic_state.shap...  66 us
    unnamed x1, local copies, waits for them, and re-layouts  1.72 us

profile of v1, /device:TPU:1, one launch (start us, length us, event | category | flops | bytes accessed | tf_op | source)
XLA Modules:
  0.0 67.8 jit_solution(11198467260296746975)
XLA Ops:
  0.0 66.0 %acoustic_steps.1 = f32[5,8,16,128]{3,2,1,0:T(8,128)} custom-call(s32[2]{0:T(128)} %offset_hbm.1, s32[2,8]{1,0:T(2,128)} %shift_hbm.1, s32[2,8]{1,0:T(2,128)} %start_hbm.1, f32[2,8]{1,0:T(2,128)} %fraction_hbm.1, f32[3,16,128]{2,1,0:T(8,128)} %flow_hbm.1, f32[5,8,16,128]{3,2,1,0:T(8,128)} %state_hbm.1), custom_call_target="tpu_custom_call" | custom-call | tf_op jit(solution)/shard_map/acoustic_steps/pallas_call | solution.py:437
  66.0 1.7 %copy.8 = f32[5,8,16,128]{3,2,1,0:T(8,128)} copy(f32[5,8,16,128]{3,2,1,0:T(8,128)} %acoustic_steps.1) | data formatting | bytes 655360

commit v2 on v1

--- a/solution.py
+++ b/solution.py
@@ -27,10 +27,10 @@
     return [spread, dx[4], dr[4], da[4], spread]
 
 
-def kernel(offset_hbm, shift_hbm, start_hbm, fraction_hbm, flow_hbm, state_hbm, out_hbm,
+def kernel(offset_hbm, shift_hbm, start_hbm, fraction_hbm, flow_hbm, state_hbm, out_hbm, fix_hbm,
            offset_ref, shift_ref, start_ref, fraction_ref,
            E, mid, slot_a0, slot_a1, slot_z0, slot_z1, slot_y0, slot_y1, slot_x0, slot_x1, facing, own_coef, flow, flow_pack,
-           own_pack, face_pad, slope, face_mid, own_fix, next_pack, fix_pad,
+           own_pack, face_pad, slope, face_mid, own_fix, next_pack, fix_pad, wide_fix,
            send_sem, recv_sem, fixed_send, fixed_recv, local_sem):
     slots_a, slots_z, slots_y, slots_x = (slot_a0, slot_a1), (slot_z0, slot_z1), (slot_y0, slot_y1), (slot_x0, slot_x1)
     i = lax.axis_index("azim")
@@ -38,6 +38,7 @@
     core, z, y, x = i % 2, (i // 2) % NZ, (i // 16) % NY, i // 64
     row0 = pl.multiple_of(8 + 8 * r, 8)
     far0 = pl.multiple_of(8 + 16 * r, 8)
+    far0_here = pl.multiple_of(24 - 16 * r, 8)
     up, down = (i + 1) % N, (i + N - 1) % N
 
     def at(azim, rad=None):
@@ -75,20 +76,16 @@
         pl.semaphore_signal(barrier, inc=1, device_id=partner, device_id_type=MESH)
 
     edge = jnp.zeros((5, 16, 8, 128), F32)
-    corner = jnp.zeros((5, 4, 8, 128), F32)
     for n in range(2):
         E[n, :, 4:20, 0:8, :] = edge
         E[n, :, 4:20, 32:40, :] = edge
-        far_own = pl.multiple_of(24 - 16 * r, 8)
-        E[n, :, 0:4, pl.ds(far_own, 8), :] = corner
-        E[n, :, 20:24, pl.ds(far_own, 8), :] = corner
     for low in (0, 32):
         mid[:, :, low:low + 8, :] = edge
         face_pad[:, :, low:low + 8, :] = jnp.zeros((5, 2, 8, 128), F32)
         fix_pad[:, low:low + 8, :] = jnp.zeros((5, 8, 128), F32)
 
     lane = lanes()
-    cell_of = lane // 16
+    cell_of = (lane // 16 + 4) % 8
     upper = lane % 16 >= 8
     row = lax.broadcasted_iota(jnp.int32, (8, 128), 0)
 
@@ -111,7 +108,7 @@
         rows = pl.ds(pl.multiple_of(row0 + 8 * t, 8), 8)
         packed = None
         for a in range(8):
-            turned = moved(E[n, f, 8 + a, rows, :], 56 - 16 * a)
+            turned = moved(E[n, f, 8 + a, rows, :], 56 - 16 * ((a + 4) % 8))
             packed = turned if packed is None else jnp.where(cell_of == a, turned, packed)
         return packed
 
@@ -142,56 +139,54 @@
     ahead = [jnp.where(half + j < 64, STENCIL[j - 1], 0.0) for j in range(1, 5)]
     behind = [jnp.where(half - j >= 0, STENCIL[j - 1], 0.0) for j in range(1, 5)]
 
-    def tall(v):
-        return jnp.concatenate([v, v, v], axis=0)
-
-    in_ahead = [tall(jnp.where(strip % 8 + j < 8, STENCIL[j - 1], 0.0)) for j in range(1, 5)]
-    in_behind = [tall(jnp.where(strip % 8 - j >= 0, STENCIL[j - 1], 0.0)) for j in range(1, 5)]
-    cross_ahead = [tall(jnp.where((strip < 8) & (strip + j >= 8), STENCIL[j - 1], 0.0)) for j in range(1, 5)]
-    cross_behind = [tall(jnp.where((strip >= 8) & (strip - j < 8), STENCIL[j - 1], 0.0)) for j in range(1, 5)]
-    lane24 = lanes(24)
+    in_ahead = [jnp.where(strip % 8 + j < 8, STENCIL[j - 1], 0.0) for j in range(1, 5)]
+    in_behind = [jnp.where(strip % 8 - j >= 0, STENCIL[j - 1], 0.0) for j in range(1, 5)]
+    cross_ahead = [jnp.where((strip < 8) & (strip + j >= 8), STENCIL[j - 1], 0.0) for j in range(1, 5)]
+    cross_behind = [jnp.where((strip >= 8) & (strip - j < 8), STENCIL[j - 1], 0.0) for j in range(1, 5)]
 
     def taps(value, fore, aft):
         total = None
         for j in range(1, 5):
-            term = fore[j - 1] * moved(value, j) - aft[j - 1] * moved(value, -j)
+            term = fore[j - 1][0:1] * moved(value, j) - aft[j - 1][0:1] * moved(value, -j)
             total = term if total is None else total + term
         return total
 
     def ring(sectors):
-        turned = [moved(v, 64) for v in sectors]
-        low = lanes(turned[0].shape[0]) < 64
-        return [jnp.where(low, turned[p], turned[(p + 1) % 3]) for p in range(3)]
+        low = lanes(sectors[0].shape[0]) < 64
+        return [jnp.where(low, sectors[p], sectors[(p + 1) % 3]) for p in range(3)]
 
     def by_cells(packs, d):
         if d == 0:
             return packs[:2]
+        at_lane = lanes(packs[0].shape[0])
         turned = [moved(v, 16 * d) for v in packs]
         if d > 0:
-            return [jnp.where(lane24 < 128 - 16 * d, turned[p], turned[p + 1]) for p in range(2)]
-        return [jnp.where(lane24 >= -16 * d, turned[p], turned[(p + 2) % 3]) for p in range(2)]
-
-    def between(packs, o):
-        if o % 8 == 0:
-            return packs[o // 8]
-        return jnp.where(lane24 < 128 - 16 * o, moved(packs[0], 16 * o), moved(packs[1], 16 * o))
-
-    def evaluate_rows(ref, c, t):
-        low = 8 + 8 * t
+            return [jnp.where(at_lane < 128 - 16 * d, turned[p], turned[p + 1]) for p in range(2)]
+        return [jnp.where(at_lane >= -16 * d, turned[p], turned[(p + 2) % 3]) for p in range(2)]
+
+    def own_cells(packs, d):
+        at_lane = lanes(packs[0].shape[0])
+        first, last = (moved(v, 16 * d) for v in packs)
+        if d >= 0:
+            return jnp.where((at_lane >= 64) & (at_lane < 128 - 16 * d), first, last)
+        return jnp.where((at_lane < 64) & (at_lane >= -16 * d), last, first)
+
+    def evaluate_rows(ref, c, low):
         dx, dr, da, mine = [], [], [], []
+        rows = pl.ds(low, 8)
         for f in range(5):
-            here = ref[f, c, low:low + 8, :]
+            here = ref[f, c, rows, :]
             mine.append(here)
             dx.append(taps(here, ahead, behind))
             radial = azimuthal = None
             for j in range(1, 5):
-                step = STENCIL[j - 1] * (ref[f, c, low + j:low + j + 8, :] - ref[f, c, low - j:low - j + 8, :])
+                step = STENCIL[j - 1] * (ref[f, c, pl.ds(low + j, 8), :] - ref[f, c, pl.ds(low - j, 8), :])
                 radial = step if radial is None else radial + step
-                step = STENCIL[j - 1] * (ref[f, c + j, low:low + 8, :] - ref[f, c - j, low:low + 8, :])
+                step = STENCIL[j - 1] * (ref[f, c + j, rows, :] - ref[f, c - j, rows, :])
                 azimuthal = step if azimuthal is None else azimuthal + step
             dr.append(radial)
             da.append(azimuthal)
-        u = [flow[k, 8 * t:8 * t + 8, :] for k in range(3)]
+        u = [flow[k, pl.ds(pl.multiple_of(low - 8, 8), 8), :] for k in range(3)]
         push = forcing(dx, dr, da)
         return mine, [-(u[0] * dx[f] + u[1] * dr[f] + u[2] * da[f]) - push[f] for f in range(5)]
 
@@ -202,8 +197,12 @@
             total = part if total is None else total + part
         return total
 
-    def own_rows_of(value, t):
-        return jnp.where(r == 0, value[8 * t:8 * t + 8], value[8 * t + 8:8 * t + 16])
+    def own_rows_of(value):
+        return jnp.where(r == 0, value[0:16], value[8:24])
+
+    def widened(f, t, a):
+        change = own_fix[f, 0, 8 * t:8 * t + 8, :]
+        return jnp.where((lane >= 56) & (lane < 72), moved(change, 16 * ((a + 4) % 8) - 56), 0.0)
 
     def step(n):
         slot_a, slot_z, slot_y, slot_x = slots_a[n], slots_z[n], slots_y[n], slots_x[n]
@@ -239,11 +238,9 @@
         else:
             def into_rows(f, carry):
                 for t in range(2):
-                    change = own_rows_of(own_fix[f, 0], t)
                     rows = pl.ds(pl.multiple_of(row0 + 8 * t, 8), 8)
                     for a in range(8):
-                        E[1, f, 8 + a, rows, :] = E[1, f, 8 + a, rows, :] + jnp.where(
-                            (lane >= 56) & (lane < 72), moved(change, 16 * a - 56), 0.0)
+                        E[1, f, 8 + a, rows, :] = E[1, f, 8 + a, rows, :] + widened(f, t, a)
                 return carry
 
             lax.fori_loop(0, 5, into_rows, 0)
@@ -282,19 +279,27 @@
                 packed = None
                 for a in range(8):
                     turned = moved(flow[m], 56 - 16 * a)
-                    packed = turned if packed is None else jnp.where(lane24 // 16 == a, turned, packed)
+                    packed = turned if packed is None else jnp.where(lanes(24) // 16 == a, turned, packed)
                 flow_pack[m] = packed
         for copy in halos:
             copy.wait_recv()
 
+        def midpoint(c, low):
+            here, slopes = evaluate_rows(E.at[n], c + 4, low)
+            for f in range(5):
+                mid[f, c, pl.ds(low, 8), :] = here[f] + (0.5 * STEP_SIZE) * slopes[f]
+
         def first(c, carry):
-            for t in range(3):
-                here, slopes = evaluate_rows(E.at[n], c + 4, t)
-                for f in range(5):
-                    mid[f, c, 8 + 8 * t:16 + 8 * t, :] = here[f] + (0.5 * STEP_SIZE) * slopes[f]
+            midpoint(c, row0)
+            midpoint(c, pl.multiple_of(row0 + 8, 8))
             return carry
 
+        def first_far(c, carry):
+            midpoint(c + 4, far0_here)
+            return carry
+
         lax.fori_loop(0, 16, first, 0)
+        lax.fori_loop(0, 8, first_far, 0)
         for copy in stage:
             copy.wait_recv()
 
@@ -310,135 +315,129 @@
         stage.append(send(facing.at[n, 1, pl.ds(5, 5)], facing.at[n, 1, rows5], at(i, 1 - r)))
 
         def second(c, carry):
-            after = []
-            for t in range(3):
-                _, slopes = evaluate_rows(mid, c + 4, t)
-                after.append([E[n, f, c + 8, 8 + 8 * t:16 + 8 * t, :] + STEP_SIZE * slopes[f] for f in range(5)])
             for t in range(2):
+                low = pl.multiple_of(row0 + 8 * t, 8)
+                _, slopes = evaluate_rows(mid, c + 4, low)
                 for f in range(5):
-                    own = jnp.where(r == 0, after[t][f], after[t + 1][f])
-                    E[n + 1, f, c + 8, pl.ds(pl.multiple_of(row0 + 8 * t, 8), 8), :] = own
+                    E[n + 1, f, c + 8, pl.ds(low, 8), :] = E[n, f, c + 8, pl.ds(low, 8), :] + STEP_SIZE * slopes[f]
             return carry
 
         lax.fori_loop(0, 8, second, 0)
+        if n == 1:
+            pltpu.make_async_copy(*result, local_sem.at[0]).start()
 
         def strip_of(f, carry):
             for p in range(3):
                 packed = None
                 for a in range(8):
-                    turned = moved(E[n, f, (4 + 8 * p + a) % 24, 8:32, :], 56 - 16 * a)
-                    packed = turned if packed is None else jnp.where(lane24 // 16 == a, turned, packed)
+                    turned = moved(E[n, f, (4 + 8 * p + a) % 24, own_rows, :], 56 - 16 * a)
+                    packed = turned if packed is None else jnp.where(lanes(16) // 16 == a, turned, packed)
                 own_pack[f, p] = packed
             if n == 0:
                 for t in range(2):
-                    next_pack[t, f] = pack_rows(1, t, f)
+                    next_pack[f, 8 * t:8 * t + 8, :] = pack_rows(1, t, f)
             return carry
 
         lax.fori_loop(0, 5, strip_of, 0)
         coef_own = ring([own_coef[p, n] for p in range(3)])
+        u24 = [flow_pack[m] for m in range(3)]
+        u = [flow_pack[m, pl.ds(pl.multiple_of(8 * r, 8), 16), :] for m in range(3)]
         for copy in stage:
             copy.wait_recv()
 
         coef_face = ring([jnp.where(upper, moved(facing[n, p, 15], -8), moved(facing[n, p, 15], 8)) for p in range(3)])
 
-        def strip_slopes(f, carry):
+        for f in range(5):
             F = ring([jnp.concatenate([facing[n, p, 5 * t + f] for t in range(3)], axis=0) for p in range(3)])
             M = [own_pack[f, p] for p in range(3)]
+            F_own = [own_rows_of(v) for v in F]
             for p in range(2):
                 face_pad[f, p, 8:32, :] = F[p]
             ghost_own = [jnp.zeros((24, 128), F32)] * 2
-            ghost_face = [jnp.zeros((24, 128), F32)] * 2
-            azimuthal = [jnp.zeros((24, 128), F32)] * 2
+            ghost_face = [jnp.zeros((16, 128), F32)] * 2
+            azimuthal = [jnp.zeros((16, 128), F32)] * 2
             for d in range(-4, 5):
-                shifted = by_cells(F, d)
+                shifted = by_cells(F if d < 4 else F_own, d)
                 if d < 4:
                     shifted_own = by_cells(M, d)
                 for p in range(2):
                     if d != 0:
                         weight = STENCIL[d - 1] if d > 0 else -STENCIL[-d - 1]
-                        azimuthal[p] = azimuthal[p] + weight * shifted[p]
+                        azimuthal[p] = azimuthal[p] + weight * (own_rows_of(shifted[p]) if d < 4 else shifted[p])
                     if d < 4:
                         ghost_own[p] = ghost_own[p] + coef_own[p][d + 4:d + 5, :] * shifted[p]
                         ghost_face[p] = ghost_face[p] + coef_face[p][d + 4:d + 5, :] * shifted_own[p]
             for p in range(2):
-                slope[0, f, p] = taps(F[p], in_ahead, in_behind) + taps(ghost_face[p], cross_ahead, cross_behind)
-                slope[1, f, p] = radial_of(face_pad, f, p)
+                slope[0, f, p] = taps(F_own[p], in_ahead, in_behind) + taps(ghost_face[p], cross_ahead, cross_behind)
+                slope[1, f, p] = own_rows_of(radial_of(face_pad, f, p))
                 slope[2, f, p] = azimuthal[p]
                 own_fix[f, p] = taps(ghost_own[p], cross_ahead, cross_behind)
-            return carry
-
-        lax.fori_loop(0, 5, strip_slopes, 0)
-
-        u = [flow_pack[m] for m in range(3)]
+
         for p in range(2):
             dx, dr, da = ([slope[m, f, p] for f in range(5)] for m in range(3))
             push = forcing(dx, dr, da)
             for f in range(5):
                 change = -(u[0] * dx[f] + u[1] * dr[f] + u[2] * da[f]) - push[f]
-                face_mid[f, p] = face_pad[f, p, 8:32, :] + (0.5 * STEP_SIZE) * change
+                face_mid[f, p] = face_pad[f, p, own_rows, :] + (0.5 * STEP_SIZE) * change
             cut = [own_fix[f, p] for f in range(5)]
             push = [cut[1], cut[4], 0.0, 0.0, cut[1]]
             for f in range(5):
-                own_fix[f, p] = (-0.5 * STEP_SIZE) * (u[0] * cut[f] + push[f])
-
-        def fix_slopes(f, carry):
+                own_fix[f, p] = (-0.5 * STEP_SIZE) * (u24[0] * cut[f] + push[f])
+
+        for f in range(5):
             face = [face_mid[f, p] for p in range(2)]
-            fix = [own_fix[f, p] for p in range(2)]
-            ghosts = jnp.zeros((24, 128), F32)
-            azimuthal = jnp.zeros((24, 128), F32)
-            for o in range(9):
-                if o < 8:
-                    ghosts = ghosts + own_coef[1, n, o:o + 1, :] * between(face, o)
-                if o != 4:
-                    weight = STENCIL[o - 5] if o > 4 else -STENCIL[3 - o]
-                    azimuthal = azimuthal + weight * between(fix, o)
-            here = between(fix, 4)
-            fix_pad[f, 8:32, :] = here
-            slope[0, f, 0] = taps(here, in_ahead, in_behind) + taps(ghosts, cross_ahead, cross_behind)
-            slope[1, f, 0] = radial_of(fix_pad, f)
+            fix = [own_rows_of(own_fix[f, p]) for p in range(2)]
+            fix_pad[f, 8:32, :] = own_cells([own_fix[f, p] for p in range(2)], 0)
+            ghosts = jnp.zeros((16, 128), F32)
+            azimuthal = jnp.zeros((16, 128), F32)
+            for d in range(-4, 5):
+                if d < 4:
+                    ghosts = ghosts + own_coef[1, n, d + 4:d + 5, :] * own_cells(face, d)
+                if d != 0:
+                    weight = STENCIL[d - 1] if d > 0 else -STENCIL[-d - 1]
+                    azimuthal = azimuthal + weight * own_cells(fix, d)
+            slope[0, f, 0] = taps(own_cells(fix, 0), in_ahead, in_behind) + taps(ghosts, cross_ahead, cross_behind)
+            slope[1, f, 0] = own_rows_of(radial_of(fix_pad, f))
             slope[2, f, 0] = azimuthal
-            return carry
-
-        lax.fori_loop(0, 5, fix_slopes, 0)
         dx, dr, da = ([slope[m, f, 0] for f in range(5)] for m in range(3))
         push = forcing(dx, dr, da)
         for f in range(5):
             change = -STEP_SIZE * (u[0] * dx[f] + u[1] * dr[f] + u[2] * da[f] + push[f])
-            own_fix[f, 0] = change
+            own_fix[f, 0, 0:16, :] = change
             if n == 0:
                 for t in range(2):
-                    slots_a[1][2 + core, 5 * t + f] = next_pack[t, f] + own_rows_of(change, t)
+                    rows = slice(8 * t, 8 * t + 8)
+                    slots_a[1][2 + core, 5 * t + f] = next_pack[f, rows, :] + change[rows]
         return started
 
+    result = (E.at[2, :, pl.ds(8, 8), pl.ds(row0, 16), :], out_hbm)
     started = step(0)
     started += step(1)
 
-    def into_result(f, carry):
+    def into_fix(f, carry):
         for t in range(2):
-            change = own_rows_of(own_fix[f, 0], t)
-            rows = pl.ds(pl.multiple_of(row0 + 8 * t, 8), 8)
             for a in range(8):
-                E[2, f, 8 + a, rows, :] = E[2, f, 8 + a, rows, :] + jnp.where(
-                    (lane >= 56) & (lane < 72), moved(change, 16 * a - 56), 0.0)
+                wide_fix[f, a, 8 * t:8 * t + 8, :] = widened(f, t, a)
         return carry
 
-    lax.fori_loop(0, 5, into_result, 0)
-    store = pltpu.make_async_copy(E.at[2, :, pl.ds(8, 8), pl.ds(row0, 16), :], out_hbm, local_sem.at[0])
-    store.start()
+    lax.fori_loop(0, 5, into_fix, 0)
+    store_fix = pltpu.make_async_copy(wide_fix, fix_hbm, local_sem.at[1])
+    store_fix.start()
     for copy in started:
         copy.wait_send()
-    store.wait()
+    pltpu.make_async_copy(*result, local_sem.at[0]).wait()
+    store_fix.wait()
 
 
 def shards(acoustic_state, mean_flow, sector_offset, cell_shift, stencil_start, interface_fraction):
     anywhere = pl.BlockSpec(memory_space=pl.ANY)
     vmem = lambda *shape: pltpu.VMEM(shape, F32)
     smem = lambda value: pltpu.SMEM(value.shape, value.dtype)
-    return pl.pallas_call(
+    without, ghosts = pl.pallas_call(
         kernel,
-        out_shape=jax.ShapeDtypeStruct(acoustic_state.shape, F32),
+        out_shape=[jax.ShapeDtypeStruct(acoustic_state.shape, F32)] * 2,
         in_specs=[anywhere] * 6,
-        out_specs=anywhere,
+        out_specs=[anywhere] * 2,
         scratch_shapes=[
             smem(sector_offset),
             smem(cell_shift),
@@ -451,13 +450,14 @@
             vmem(3, 2, 8, 128),
             vmem(3, 24, 128),
             vmem(3, 24, 128),
-            vmem(5, 3, 24, 128),
+            vmem(5, 3, 16, 128),
             vmem(5, 2, 40, 128),
-            vmem(3, 5, 2, 24, 128),
+            vmem(3, 5, 2, 16, 128),
+            vmem(5, 2, 16, 128),
             vmem(5, 2, 24, 128),
-            vmem(5, 2, 24, 128),
-            vmem(2, 5, 8, 128),
+            vmem(5, 16, 128),
             vmem(5, 40, 128),
+            vmem(5, 8, 16, 128),
             pltpu.SemaphoreType.DMA((2, 24)),
             pltpu.SemaphoreType.DMA((2, 24)),
             pltpu.SemaphoreType.DMA((3,)),
@@ -467,6 +467,7 @@
         compiler_params=pltpu.CompilerParams(collective_id=0, has_side_effects=True, vmem_limit_bytes=67043328),
         name="acoustic_steps",
     )(sector_offset, cell_shift, stencil_start, interface_fraction, mean_flow, acoustic_state)
+    return without + ghosts
 
 
 def solution(mesh):

time: 68.2 us -> 66.2 us (0.971)
  Pallas kernels: 66 us -> 63.5 us
  other arithmetic: 0 us -> 1.84 us
  local copies, waits for them, and re-layouts: 1.72 us -> 0 us
    pallas_call x1, Pallas kernels: 66 us -> 63.5 us  [shards(): pl.pallas_call(kernel, out_shape=[jax.ShapeDtypeStruct(acoustic_state.sha...]
    add x0 -> x1, other arithmetic: none -> 1.84 us  [shards(): return without + ghosts]
    unnamed x1 -> x0, local copies, waits for them, and re-layouts: 1.72 us -> none
where the time goes in v2:
time: 66.2 us; the launch traced here: 65.4 us
  Pallas kernels  63.5 us (96%)
  other arithmetic  1.84 us (3%)
    pallas_call x1, Pallas kernels, shards(): pl.pallas_call(kernel, out_shape=[jax.ShapeDtypeStruct(acoustic_state.sha...  63.5 us
    add x1, other arithmetic, shards(): return without + ghosts  1.84 us

profile of v2, /device:TPU:1, one launch (start us, length us, event | category | flops | bytes accessed | tf_op | source)
XLA Modules:
  0.0 65.4 jit_solution(15609402692770634417)
XLA Ops:
  0.0 63.5 %acoustic_steps.1 = (f32[5,8,16,128]{3,2,1,0:T(8,128)}, f32[5,8,16,128]{3,2,1,0:T(8,128)}) custom-call(s32[2]{0:T(128)} %offset_hbm.1, s32[2,8]{1,0:T(2,128)} %shift_hbm.1, s32[2,8]{1,0:T(2,128)} %start_hbm.1, f32[2,8]{1,0:T(2,128)} %fraction_hbm.1, f32[3,16,128]{2,1,0:T(8,128)} %flow_hbm.1, f32[5,8,16,128]{3,2,1,0:T(8,128)} %state_hbm.1), custom_call_target="tpu_custom_call" | custom-call | tf_op jit(solution)/shard_map/acoustic_steps/pallas_call | solution.py:436
  63.5 1.8 %add.3 = f32[5,8,16,128]{3,2,1,0:T(8,128)} add(f32[5,8,16,128]{3,2,1,0:T(8,128)} %get-tuple-element.7, f32[5,8,16,128]{3,2,1,0:T(8,128)} %get-tuple-element.8) | non-fusion elementwise | flops 81920 | bytes 983040 | tf_op jit(solution)/shard_map/add | solution.py:470

commit v3 on v2

--- a/solution.py
+++ b/solution.py
@@ -29,10 +29,11 @@
 
 def kernel(offset_hbm, shift_hbm, start_hbm, fraction_hbm, flow_hbm, state_hbm, out_hbm, fix_hbm,
            offset_ref, shift_ref, start_ref, fraction_ref,
-           E, mid, slot_a0, slot_a1, slot_z0, slot_z1, slot_y0, slot_y1, slot_x0, slot_x1, facing, own_coef, flow, flow_pack,
+           E, mid, near_a0, near_a1, near_b0, near_b1, far_a0, far_a1, far_b0, far_b1, y_a0, y_a1, y_b0, y_b1, x_a0, x_a1, x_b0, x_b1, facing, own_coef, flow, flow_pack,
            own_pack, face_pad, slope, face_mid, own_fix, next_pack, fix_pad, wide_fix,
            send_sem, recv_sem, fixed_send, fixed_recv, local_sem):
-    slots_a, slots_z, slots_y, slots_x = (slot_a0, slot_a1), (slot_z0, slot_z1), (slot_y0, slot_y1), (slot_x0, slot_x1)
+    near_a, near_b, far_a, far_b = (near_a0, near_a1), (near_b0, near_b1), (far_a0, far_a1), (far_b0, far_b1)
+    ys_a, ys_b, xs_a, xs_b = (y_a0, y_a1), (y_b0, y_b1), (x_a0, x_a1), (x_b0, x_b1)
     i = lax.axis_index("azim")
     r = lax.axis_index("rad")
     core, z, y, x = i % 2, (i // 2) % NZ, (i // 16) % NY, i // 64
@@ -114,16 +115,16 @@
 
     for copy in loads:
         copy.wait()
-    for t in range(2):
-        for f in range(5):
-            slots_a[0][2 + core, t * 5 + f] = pack_rows(0, t, f)
+    for f in range(5):
+        near_a[0][2 + core, f] = pack_rows(0, 0, f)
+        ys_b[0][y, f] = pack_rows(0, 1, f)
     stator_t = spread_cells(lambda a: fraction_ref[0, a])
     rotor_t = spread_cells(lambda a: fraction_ref[1, a])
     for n in range(2):
         stator = weights(stator_t, row - spread_cells(lambda a: shift_ref[n, a] + start_ref[0, a] + 3))
         rotor = weights(rotor_t, row - spread_cells(lambda a: start_ref[1, a] - shift_ref[n, a]))
         own_coef[1, n] = jnp.where(upper, stator, rotor)
-        slots_a[n][2 + core, 10] = jnp.where(upper, rotor, stator)
+        near_a[n][2 + core, 5] = jnp.where(upper, rotor, stator)
 
     pl.semaphore_wait(barrier, len(partners))
     fixed = []
@@ -205,7 +206,6 @@
         return jnp.where((lane >= 56) & (lane < 72), moved(change, 16 * ((a + 4) % 8) - 56), 0.0)
 
     def step(n):
-        slot_a, slot_z, slot_y, slot_x = slots_a[n], slots_z[n], slots_y[n], slots_x[n]
         k = offset_ref[n]
         source_r = (i - k + N) % N
         source_s = (i + k) % N
@@ -228,8 +228,25 @@
         def chosen(slots, from_r, from_s):
             return jnp.where(upper[None], slots[from_r], slots[from_s])
 
-        mine = slot_a.at[2 + core]
-        stage = [send(mine, slot_a.at[place], at(j)) for j, place in near_to]
+        def along(slots, own, targets):
+            mine = slots.at[own]
+            return [send(mine, slots.at[place], at(j)) for j, place in targets]
+
+        def arrived(copies):
+            for copy in copies:
+                copy.wait_recv()
+
+        low = i % 16
+        high = i // 16
+        high_r = (high - k // 16 - (low + k % 16) // 16 + 16) % 8
+        high_s = (high + k // 16 + (k % 16 + 15 - low) // 16) % 8
+        (near_r, far_r), (near_s, far_s) = parts(low_r), parts(low_s)
+        near_of = (2 * (near_r + 1) + low_r % 2, 2 * (near_s + 1) + low_s % 2)
+        ys = [(j, y) for j in y_to]
+        xs = [(x_to, x)]
+
+        stage_a = along(near_a[n], 2 + core, near_to)
+        stage_b = along(ys_b[n], y, ys)
 
         if n == 0:
             send_fixed(own_coef.at[1], own_coef.at[0], at(up))
@@ -247,30 +264,38 @@
 
         own_rows, far_rows = pl.ds(row0, 16), pl.ds(far0, 8)
         halos = []
+
+        def halo_cells(fields):
+            part = E.at[n, fields, pl.ds(8, 8), own_rows, :]
+            halos.append(send(part, E.at[n, fields, pl.ds(0, 8), own_rows, :], at(up)))
+            halos.append(send(part, E.at[n, fields, pl.ds(16, 8), own_rows, :], at(down)))
+
         halos.append(send(E.at[n, :, pl.ds(8, 8), pl.ds(16, 8), :], E.at[n, :, pl.ds(8, 8), far_rows, :], at(i, 1 - r)))
+        halo_cells(pl.ds(0, 2))
+        arrived(stage_a)
+        far_a[n][1] = chosen(near_a[n], *near_of)
+        stage_a = along(far_a[n], 1, z_to)
+        arrived(stage_b)
+        xs_b[n][x] = chosen(ys_b[n], high_r % NY, high_s % NY)
+        stage_b = along(xs_b[n], x, xs)
+        halo_cells(pl.ds(2, 1))
+
+        arrived(stage_b)
+        near_b[n][2 + core] = chosen(xs_b[n], high_r // NY, high_s // NY)
+        stage_b = along(near_b[n], 2 + core, near_to)
         halos.append(send(E.at[n, :, pl.ds(12, 4), pl.ds(16, 8), :], E.at[n, :, pl.ds(4, 4), far_rows, :], at(up, 1 - r)))
         halos.append(send(E.at[n, :, pl.ds(8, 4), pl.ds(16, 8), :], E.at[n, :, pl.ds(16, 4), far_rows, :], at(down, 1 - r)))
-        for copy in stage:
-            copy.wait_recv()
-
-        (near_r, far_r), (near_s, far_s) = parts(low_r), parts(low_s)
-        slot_z[1] = chosen(slot_a, 2 * (near_r + 1) + low_r % 2, 2 * (near_s + 1) + low_s % 2)
-        mine = slot_z.at[1]
-        stage = [send(mine, slot_z.at[place], at(j)) for j, place in z_to]
-        halos.append(send(E.at[n, :, pl.ds(8, 8), own_rows, :], E.at[n, :, pl.ds(0, 8), own_rows, :], at(up)))
-        halos.append(send(E.at[n, :, pl.ds(8, 8), own_rows, :], E.at[n, :, pl.ds(16, 8), own_rows, :], at(down)))
-        for copy in stage:
-            copy.wait_recv()
-
-        slot_y[y] = chosen(slot_z, far_r + 1, far_s + 1)
-        mine = slot_y.at[y]
-        stage = [send(mine, mine, at(j)) for j in y_to]
-        for copy in stage:
-            copy.wait_recv()
-
-        slot_x[x] = chosen(slot_y, (source_r // 16) % NY, (source_s // 16) % NY)
-        mine = slot_x.at[x]
-        stage = [send(mine, mine, at(x_to))]
+        arrived(stage_a)
+        ys_a[n][y] = chosen(far_a[n], far_r + 1, far_s + 1)
+        stage_a = along(ys_a[n], y, ys)
+        halo_cells(pl.ds(3, 2))
+
+        arrived(stage_b)
+        far_b[n][1] = chosen(near_b[n], *near_of)
+        stage_b = along(far_b[n], 1, z_to)
+        arrived(stage_a)
+        xs_a[n][x] = chosen(ys_a[n], (source_r // 16) % NY, (source_s // 16) % NY)
+        stage_a = along(xs_a[n], x, xs)
 
         if n == 0:
             for copy in fixed:
@@ -300,12 +325,12 @@
 
         lax.fori_loop(0, 16, first, 0)
         lax.fori_loop(0, 8, first_far, 0)
-        for copy in stage:
-            copy.wait_recv()
-
-        got = chosen(slot_x, source_r // 64, source_s // 64)
-        facing[n, 1, pl.ds(5 * r, 10)] = got[0:10]
-        facing[n, 1, 15] = got[10]
+        arrived(stage_a)
+        got = chosen(xs_a[n], source_r // 64, source_s // 64)
+        facing[n, 1, pl.ds(5 * r, 5)] = got[0:5]
+        facing[n, 1, 15] = got[5]
+        arrived(stage_b)
+        facing[n, 1, pl.ds(5 * r + 5, 5)] = chosen(far_b[n], far_r + 1, far_s + 1)
         rows10, rows5 = pl.ds(5 * r, 10), pl.ds(10 * r, 5)
         stage = []
         for to, place in ((up, 0), (down, 2)):
@@ -405,9 +430,9 @@
             change = -STEP_SIZE * (u[0] * dx[f] + u[1] * dr[f] + u[2] * da[f] + push[f])
             own_fix[f, 0, 0:16, :] = change
             if n == 0:
-                for t in range(2):
-                    rows = slice(8 * t, 8 * t + 8)
-                    slots_a[1][2 + core, 5 * t + f] = next_pack[f, rows, :] + change[rows]
+                after = next_pack[f] + change
+                near_a[1][2 + core, f] = after[0:8]
+                ys_b[1][y, f] = after[8:16]
         return started
 
     result = (E.at[2, :, pl.ds(8, 8), pl.ds(row0, 16), :], out_hbm)
@@ -445,7 +470,7 @@
             smem(interface_fraction),
             vmem(3, 5, 24, 40, 128),
             vmem(5, 16, 40, 128),
-            *[vmem(count, 11, 8, 128) for count in (6, 3, NY, NX) for _ in range(2)],
+            *[vmem(count, tiles, 8, 128) for count in (6, 3, NY, NX) for tiles in (6, 5) for _ in range(2)],
             vmem(2, 3, 16, 8, 128),
             vmem(3, 2, 8, 128),
             vmem(3, 24, 128),
@@ -458,8 +483,8 @@
             vmem(5, 16, 128),
             vmem(5, 40, 128),
             vmem(5, 8, 16, 128),
-            pltpu.SemaphoreType.DMA((2, 24)),
-            pltpu.SemaphoreType.DMA((2, 24)),
+            pltpu.SemaphoreType.DMA((2, 40)),
+            pltpu.SemaphoreType.DMA((2, 40)),
             pltpu.SemaphoreType.DMA((3,)),
             pltpu.SemaphoreType.DMA((3,)),
             pltpu.SemaphoreType.DMA((6,)),

time: 66.2 us -> 66.1 us (level)
  the two profiles are of different devices: /device:TPU:1 before, /device:TPU:2 now
where the time goes in v3:
time: 66.1 us; the launch traced here: 66 us
  Pallas kernels  64.2 us (97%)
  other arithmetic  1.84 us (3%)
    pallas_call x1, Pallas kernels, shards(): pl.pallas_call(kernel, out_shape=[jax.ShapeDtypeStruct(acoustic_state.sha...  64.2 us
    add x1, other arithmetic, shards(): return without + ghosts  1.84 us

profile of v3, /device:TPU:2, one launch (start us, length us, event | category | flops | bytes accessed | tf_op | source)
XLA Modules:
  0.0 66.0 jit_solution(4969878750811757032)
XLA Ops:
  0.0 64.2 %acoustic_steps.1 = (f32[5,8,16,128]{3,2,1,0:T(8,128)}, f32[5,8,16,128]{3,2,1,0:T(8,128)}) custom-call(s32[2]{0:T(128)} %offset_hbm.1, s32[2,8]{1,0:T(2,128)} %shift_hbm.1, s32[2,8]{1,0:T(2,128)} %start_hbm.1, f32[2,8]{1,0:T(2,128)} %fraction_hbm.1, f32[3,16,128]{2,1,0:T(8,128)} %flow_hbm.1, f32[5,8,16,128]{3,2,1,0:T(8,128)} %state_hbm.1), custom_call_target="tpu_custom_call" | custom-call | tf_op jit(solution)/shard_map/acoustic_steps/pallas_call | solution.py:461
  64.2 1.8 %add.3 = f32[5,8,16,128]{3,2,1,0:T(8,128)} add(f32[5,8,16,128]{3,2,1,0:T(8,128)} %get-tuple-element.7, f32[5,8,16,128]{3,2,1,0:T(8,128)} %get-tuple-element.8) | non-fusion elementwise | flops 81920 | bytes 983040 | tf_op jit(solution)/shard_map/add | solution.py:495

commit v4 on v3

--- a/solution.py
+++ b/solution.py
@@ -306,25 +306,6 @@
                     turned = moved(flow[m], 56 - 16 * a)
                     packed = turned if packed is None else jnp.where(lanes(24) // 16 == a, turned, packed)
                 flow_pack[m] = packed
-        for copy in halos:
-            copy.wait_recv()
-
-        def midpoint(c, low):
-            here, slopes = evaluate_rows(E.at[n], c + 4, low)
-            for f in range(5):
-                mid[f, c, pl.ds(low, 8), :] = here[f] + (0.5 * STEP_SIZE) * slopes[f]
-
-        def first(c, carry):
-            midpoint(c, row0)
-            midpoint(c, pl.multiple_of(row0 + 8, 8))
-            return carry
-
-        def first_far(c, carry):
-            midpoint(c + 4, far0_here)
-            return carry
-
-        lax.fori_loop(0, 16, first, 0)
-        lax.fori_loop(0, 8, first_far, 0)
         arrived(stage_a)
         got = chosen(xs_a[n], source_r // 64, source_s // 64)
         facing[n, 1, pl.ds(5 * r, 5)] = got[0:5]
@@ -339,6 +320,25 @@
             stage.append(send(facing.at[n, 1, pl.ds(5, 5)], facing.at[n, place, rows5], at(to, 1 - r)))
         stage.append(send(facing.at[n, 1, pl.ds(5, 5)], facing.at[n, 1, rows5], at(i, 1 - r)))
 
+        for copy in halos:
+            copy.wait_recv()
+
+        def midpoint(c, low):
+            here, slopes = evaluate_rows(E.at[n], c + 4, low)
+            for f in range(5):
+                mid[f, c, pl.ds(low, 8), :] = here[f] + (0.5 * STEP_SIZE) * slopes[f]
+
+        def first(c, carry):
+            midpoint(c, row0)
+            midpoint(c, pl.multiple_of(row0 + 8, 8))
+            return carry
+
+        def first_far(c, carry):
+            midpoint(c + 4, far0_here)
+            return carry
+
+        lax.fori_loop(0, 16, first, 0)
+        lax.fori_loop(0, 8, first_far, 0)
         def second(c, carry):
             for t in range(2):
                 low = pl.multiple_of(row0 + 8 * t, 8)

time: 66.1 us -> 62.7 us (0.949)
  the two profiles are of different devices: /device:TPU:2 before, /device:TPU:1 now
where the time goes in v4:
time: 62.7 us; the launch traced here: 62.1 us
  Pallas kernels  60.2 us (96%)
  other arithmetic  1.84 us (3%)
    pallas_call x1, Pallas kernels, shards(): pl.pallas_call(kernel, out_shape=[jax.ShapeDtypeStruct(acoustic_state.sha...  60.2 us
    add x1, other arithmetic, shards(): return without + ghosts  1.84 us

profile of v4, /device:TPU:1, one launch (start us, length us, event | category | flops | bytes accessed | tf_op | source)
XLA Modules:
  0.0 62.1 jit_solution(12910410094242623489)
XLA Ops:
  0.0 60.2 %acoustic_steps.1 = (f32[5,8,16,128]{3,2,1,0:T(8,128)}, f32[5,8,16,128]{3,2,1,0:T(8,128)}) custom-call(s32[2]{0:T(128)} %offset_hbm.1, s32[2,8]{1,0:T(2,128)} %shift_hbm.1, s32[2,8]{1,0:T(2,128)} %start_hbm.1, f32[2,8]{1,0:T(2,128)} %fraction_hbm.1, f32[3,16,128]{2,1,0:T(8,128)} %flow_hbm.1, f32[5,8,16,128]{3,2,1,0:T(8,128)} %state_hbm.1), custom_call_target="tpu_custom_call" | custom-call | tf_op jit(solution)/shard_map/acoustic_steps/pallas_call | solution.py:461
  60.3 1.8 %add.3 = f32[5,8,16,128]{3,2,1,0:T(8,128)} add(f32[5,8,16,128]{3,2,1,0:T(8,128)} %get-tuple-element.7, f32[5,8,16,128]{3,2,1,0:T(8,128)} %get-tuple-element.8) | non-fusion elementwise | flops 81920 | bytes 983040 | tf_op jit(solution)/shard_map/add | solution.py:495

commit v5 on v4

--- a/solution.py
+++ b/solution.py
@@ -270,7 +270,10 @@
             halos.append(send(part, E.at[n, fields, pl.ds(0, 8), own_rows, :], at(up)))
             halos.append(send(part, E.at[n, fields, pl.ds(16, 8), own_rows, :], at(down)))
 
-        halos.append(send(E.at[n, :, pl.ds(8, 8), pl.ds(16, 8), :], E.at[n, :, pl.ds(8, 8), far_rows, :], at(i, 1 - r)))
+        def halo_rows(fields):
+            halos.append(send(E.at[n, fields, pl.ds(8, 8), pl.ds(16, 8), :], E.at[n, fields, pl.ds(8, 8), far_rows, :], at(i, 1 - r)))
+
+        halo_rows(pl.ds(0, 3))
         halo_cells(pl.ds(0, 2))
         arrived(stage_a)
         far_a[n][1] = chosen(near_a[n], *near_of)
@@ -278,17 +281,18 @@
         arrived(stage_b)
         xs_b[n][x] = chosen(ys_b[n], high_r % NY, high_s % NY)
         stage_b = along(xs_b[n], x, xs)
-        halo_cells(pl.ds(2, 1))
+        halo_cells(pl.ds(2, 2))
 
         arrived(stage_b)
         near_b[n][2 + core] = chosen(xs_b[n], high_r // NY, high_s // NY)
         stage_b = along(near_b[n], 2 + core, near_to)
+        halo_rows(pl.ds(3, 2))
         halos.append(send(E.at[n, :, pl.ds(12, 4), pl.ds(16, 8), :], E.at[n, :, pl.ds(4, 4), far_rows, :], at(up, 1 - r)))
         halos.append(send(E.at[n, :, pl.ds(8, 4), pl.ds(16, 8), :], E.at[n, :, pl.ds(16, 4), far_rows, :], at(down, 1 - r)))
         arrived(stage_a)
         ys_a[n][y] = chosen(far_a[n], far_r + 1, far_s + 1)
         stage_a = along(ys_a[n], y, ys)
-        halo_cells(pl.ds(3, 2))
+        halo_cells(pl.ds(4, 1))
 
         arrived(stage_b)
         far_b[n][1] = chosen(near_b[n], *near_of)
@@ -337,8 +341,8 @@
             midpoint(c + 4, far0_here)
             return carry
 
-        lax.fori_loop(0, 16, first, 0)
-        lax.fori_loop(0, 8, first_far, 0)
+        lax.fori_loop(0, 16, first, 0, unroll=2)
+        lax.fori_loop(0, 8, first_far, 0, unroll=2)
         def second(c, carry):
             for t in range(2):
                 low = pl.multiple_of(row0 + 8 * t, 8)
@@ -347,7 +351,7 @@
                     E[n + 1, f, c + 8, pl.ds(low, 8), :] = E[n, f, c + 8, pl.ds(low, 8), :] + STEP_SIZE * slopes[f]
             return carry
 
-        lax.fori_loop(0, 8, second, 0)
+        lax.fori_loop(0, 8, second, 0, unroll=2)
         if n == 1:
             pltpu.make_async_copy(*result, local_sem.at[0]).start()
 

time: 62.7 us -> 60.1 us (0.959)
  Pallas kernels: 60.2 us -> 58.2 us
    pallas_call x1, Pallas kernels: 60.2 us -> 58.2 us  [shards(): pl.pallas_call(kernel, out_shape=[jax.ShapeDtypeStruct(acoustic_state.sha...]
where the time goes in v5:
time: 60.1 us; the launch traced here: 60 us
  Pallas kernels  58.2 us (97%)
  other arithmetic  1.84 us (3%)
    pallas_call x1, Pallas kernels, shards(): pl.pallas_call(kernel, out_shape=[jax.ShapeDtypeStruct(acoustic_state.sha...  58.2 us
    add x1, other arithmetic, shards(): return without + ghosts  1.84 us

profile of v5, /device:TPU:1, one launch (start us, length us, event | category | flops | bytes accessed | tf_op | source)
XLA Modules:
  0.0 60.0 jit_solution(1707732426567931273)
XLA Ops:
  0.0 58.2 %acoustic_steps.1 = (f32[5,8,16,128]{3,2,1,0:T(8,128)}, f32[5,8,16,128]{3,2,1,0:T(8,128)}) custom-call(s32[2]{0:T(128)} %offset_hbm.1, s32[2,8]{1,0:T(2,128)} %shift_hbm.1, s32[2,8]{1,0:T(2,128)} %start_hbm.1, f32[2,8]{1,0:T(2,128)} %fraction_hbm.1, f32[3,16,128]{2,1,0:T(8,128)} %flow_hbm.1, f32[5,8,16,128]{3,2,1,0:T(8,128)} %state_hbm.1), custom_call_target="tpu_custom_call" | custom-call | tf_op jit(solution)/shard_map/acoustic_steps/pallas_call | solution.py:465
  58.2 1.8 %add.3 = f32[5,8,16,128]{3,2,1,0:T(8,128)} add(f32[5,8,16,128]{3,2,1,0:T(8,128)} %get-tuple-element.7, f32[5,8,16,128]{3,2,1,0:T(8,128)} %get-tuple-element.8) | non-fusion elementwise | flops 81920 | bytes 983040 | tf_op jit(solution)/shard_map/add | solution.py:499

commit v6 on v5

--- a/solution.py
+++ b/solution.py
@@ -30,7 +30,7 @@
 def kernel(offset_hbm, shift_hbm, start_hbm, fraction_hbm, flow_hbm, state_hbm, out_hbm, fix_hbm,
            offset_ref, shift_ref, start_ref, fraction_ref,
            E, mid, near_a0, near_a1, near_b0, near_b1, far_a0, far_a1, far_b0, far_b1, y_a0, y_a1, y_b0, y_b1, x_a0, x_a1, x_b0, x_b1, facing, own_coef, flow, flow_pack,
-           own_pack, face_pad, slope, face_mid, own_fix, next_pack, fix_pad, wide_fix,
+           own_pack, face_pad, slope, face_mid, own_fix, next_pack, fix_pad, wide_fix, inside, across,
            send_sem, recv_sem, fixed_send, fixed_recv, local_sem):
     near_a, near_b, far_a, far_b = (near_a0, near_a1), (near_b0, near_b1), (far_a0, far_a1), (far_b0, far_b1)
     ys_a, ys_b, xs_a, xs_b = (y_a0, y_a1), (y_b0, y_b1), (x_a0, x_a1), (x_b0, x_b1)
@@ -84,6 +84,16 @@
         mid[:, :, low:low + 8, :] = edge
         face_pad[:, :, low:low + 8, :] = jnp.zeros((5, 2, 8, 128), F32)
         fix_pad[:, low:low + 8, :] = jnp.zeros((5, 8, 128), F32)
+
+    source = lax.broadcasted_iota(jnp.int32, (128, 128), 0)
+    target = lax.broadcasted_iota(jnp.int32, (128, 128), 1)
+    weight = jnp.zeros((128, 128), F32)
+    for j in range(1, 5):
+        weight = jnp.where(source - target == j, STENCIL[j - 1], jnp.where(target - source == j, -STENCIL[j - 1], weight))
+    same_cell = source // 16 == target // 16
+    same_frame = source // 8 == target // 8
+    inside[...] = jnp.where(same_frame, weight, 0.0)
+    across[...] = jnp.where(same_cell & ~same_frame, weight, 0.0)
 
     lane = lanes()
     cell_of = (lane // 16 + 4) % 8
@@ -136,14 +146,8 @@
         fixed.append(copy)
 
     half = lane % 64
-    strip = lane % 16
     ahead = [jnp.where(half + j < 64, STENCIL[j - 1], 0.0) for j in range(1, 5)]
     behind = [jnp.where(half - j >= 0, STENCIL[j - 1], 0.0) for j in range(1, 5)]
-
-    in_ahead = [jnp.where(strip % 8 + j < 8, STENCIL[j - 1], 0.0) for j in range(1, 5)]
-    in_behind = [jnp.where(strip % 8 - j >= 0, STENCIL[j - 1], 0.0) for j in range(1, 5)]
-    cross_ahead = [jnp.where((strip < 8) & (strip + j >= 8), STENCIL[j - 1], 0.0) for j in range(1, 5)]
-    cross_behind = [jnp.where((strip >= 8) & (strip - j < 8), STENCIL[j - 1], 0.0) for j in range(1, 5)]
 
     def taps(value, fore, aft):
         total = None
@@ -151,6 +155,11 @@
             term = fore[j - 1][0:1] * moved(value, j) - aft[j - 1][0:1] * moved(value, -j)
             total = term if total is None else total + term
         return total
+
+    def product(parts, matrix):
+        rows = parts[0].shape[0]
+        whole = jnp.dot(jnp.concatenate(parts, axis=0), matrix[...], precision=lax.Precision.HIGHEST, preferred_element_type=F32)
+        return [whole[rows * m:rows * m + rows] for m in range(len(parts))]
 
     def ring(sectors):
         low = lanes(sectors[0].shape[0]) < 64
@@ -376,6 +385,7 @@
 
         coef_face = ring([jnp.where(upper, moved(facing[n, p, 15], -8), moved(facing[n, p, 15], 8)) for p in range(3)])
 
+        all_face, all_ghost_own, all_ghost_face = [], [], []
         for f in range(5):
             F = ring([jnp.concatenate([facing[n, p, 5 * t + f] for t in range(3)], axis=0) for p in range(3)])
             M = [own_pack[f, p] for p in range(3)]
@@ -397,10 +407,15 @@
                         ghost_own[p] = ghost_own[p] + coef_own[p][d + 4:d + 5, :] * shifted[p]
                         ghost_face[p] = ghost_face[p] + coef_face[p][d + 4:d + 5, :] * shifted_own[p]
             for p in range(2):
-                slope[0, f, p] = taps(F_own[p], in_ahead, in_behind) + taps(ghost_face[p], cross_ahead, cross_behind)
                 slope[1, f, p] = own_rows_of(radial_of(face_pad, f, p))
                 slope[2, f, p] = azimuthal[p]
-                own_fix[f, p] = taps(ghost_own[p], cross_ahead, cross_behind)
+            all_face += F_own[:2]
+            all_ghost_own += ghost_own
+            all_ghost_face += ghost_face
+        for m, (a, b) in enumerate(zip(product(all_face, inside), product(all_ghost_face, across))):
+            slope[0, m // 2, m % 2] = a + b
+        for m, a in enumerate(product(all_ghost_own, across)):
+            own_fix[m // 2, m % 2] = a
 
         for p in range(2):
             dx, dr, da = ([slope[m, f, p] for f in range(5)] for m in range(3))
@@ -413,6 +428,7 @@
             for f in range(5):
                 own_fix[f, p] = (-0.5 * STEP_SIZE) * (u24[0] * cut[f] + push[f])
 
+        all_fix, all_ghost = [], []
         for f in range(5):
             face = [face_mid[f, p] for p in range(2)]
             fix = [own_rows_of(own_fix[f, p]) for p in range(2)]
@@ -425,10 +441,12 @@
                 if d != 0:
                     weight = STENCIL[d - 1] if d > 0 else -STENCIL[-d - 1]
                     azimuthal = azimuthal + weight * own_cells(fix, d)
-            slope[0, f, 0] = taps(own_cells(fix, 0), in_ahead, in_behind) + taps(ghosts, cross_ahead, cross_behind)
+            all_fix.append(own_cells(fix, 0))
+            all_ghost.append(ghosts)
             slope[1, f, 0] = own_rows_of(radial_of(fix_pad, f))
             slope[2, f, 0] = azimuthal
-        dx, dr, da = ([slope[m, f, 0] for f in range(5)] for m in range(3))
+        dx = [a + b for a, b in zip(product(all_fix, inside), product(all_ghost, across))]
+        dr, da = ([slope[m, f, 0] for f in range(5)] for m in range(1, 3))
         push = forcing(dx, dr, da)
         for f in range(5):
             change = -STEP_SIZE * (u[0] * dx[f] + u[1] * dr[f] + u[2] * da[f] + push[f])
@@ -487,6 +505,8 @@
             vmem(5, 16, 128),
             vmem(5, 40, 128),
             vmem(5, 8, 16, 128),
+            vmem(128, 128),
+            vmem(128, 128),
             pltpu.SemaphoreType.DMA((2, 40)),
             pltpu.SemaphoreType.DMA((2, 40)),
             pltpu.SemaphoreType.DMA((3,)),

time: 60.1 us -> 58.2 us (0.968)
  Pallas kernels: 58.2 us -> 56.3 us
    pallas_call x1, Pallas kernels: 58.2 us -> 56.3 us  [shards(): pl.pallas_call(kernel, out_shape=[jax.ShapeDtypeStruct(acoustic_state.sha...]
where the time goes in v6:
time: 58.2 us; the launch traced here: 58.1 us
  Pallas kernels  56.3 us (97%)
  other arithmetic  1.84 us (3%)
    pallas_call x1, Pallas kernels, shards(): pl.pallas_call(kernel, out_shape=[jax.ShapeDtypeStruct(acoustic_state.sha...  56.3 us
    add x1, other arithmetic, shards(): return without + ghosts  1.84 us

profile of v6, /device:TPU:1, one launch (start us, length us, event | category | flops | bytes accessed | tf_op | source)
XLA Modules:
  0.0 58.1 jit_solution(3633045434384044552)
XLA Ops:
  0.0 56.3 %acoustic_steps.1 = (f32[5,8,16,128]{3,2,1,0:T(8,128)}, f32[5,8,16,128]{3,2,1,0:T(8,128)}) custom-call(s32[2]{0:T(128)} %offset_hbm.1, s32[2,8]{1,0:T(2,128)} %shift_hbm.1, s32[2,8]{1,0:T(2,128)} %start_hbm.1, f32[2,8]{1,0:T(2,128)} %fraction_hbm.1, f32[3,16,128]{2,1,0:T(8,128)} %flow_hbm.1, f32[5,8,16,128]{3,2,1,0:T(8,128)} %state_hbm.1), custom_call_target="tpu_custom_call" | custom-call | tf_op jit(solution)/shard_map/acoustic_steps/pallas_call | solution.py:483
  56.3 1.8 %add.3 = f32[5,8,16,128]{3,2,1,0:T(8,128)} add(f32[5,8,16,128]{3,2,1,0:T(8,128)} %get-tuple-element.7, f32[5,8,16,128]{3,2,1,0:T(8,128)} %get-tuple-element.8) | non-fusion elementwise | flops 81920 | bytes 983040 | tf_op jit(solution)/shard_map/add | solution.py:519

commit v7 on v6

--- a/solution.py
+++ b/solution.py
@@ -30,7 +30,7 @@
 def kernel(offset_hbm, shift_hbm, start_hbm, fraction_hbm, flow_hbm, state_hbm, out_hbm, fix_hbm,
            offset_ref, shift_ref, start_ref, fraction_ref,
            E, mid, near_a0, near_a1, near_b0, near_b1, far_a0, far_a1, far_b0, far_b1, y_a0, y_a1, y_b0, y_b1, x_a0, x_a1, x_b0, x_b1, facing, own_coef, flow, flow_pack,
-           own_pack, face_pad, slope, face_mid, own_fix, next_pack, fix_pad, wide_fix, inside, across,
+           face_pad, slope, face_mid, own_fix, next_pack, fix_pad, wide_fix, inside, across, own_shifted,
            send_sem, recv_sem, fixed_send, fixed_recv, local_sem):
     near_a, near_b, far_a, far_b = (near_a0, near_a1), (near_b0, near_b1), (far_a0, far_a1), (far_b0, far_b1)
     ys_a, ys_b, xs_a, xs_b = (y_a0, y_a1), (y_b0, y_b1), (x_a0, x_a1), (x_b0, x_b1)
@@ -365,12 +365,16 @@
             pltpu.make_async_copy(*result, local_sem.at[0]).start()
 
         def strip_of(f, carry):
+            packs = []
             for p in range(3):
                 packed = None
                 for a in range(8):
                     turned = moved(E[n, f, (4 + 8 * p + a) % 24, own_rows, :], 56 - 16 * a)
                     packed = turned if packed is None else jnp.where(lanes(16) // 16 == a, turned, packed)
-                own_pack[f, p] = packed
+                packs.append(packed)
+            for d in range(-4, 4):
+                for p, shifted in enumerate(by_cells(packs, d)):
+                    own_shifted[f, d + 4, p] = shifted
             if n == 0:
                 for t in range(2):
                     next_pack[f, 8 * t:8 * t + 8, :] = pack_rows(1, t, f)
@@ -388,7 +392,6 @@
         all_face, all_ghost_own, all_ghost_face = [], [], []
         for f in range(5):
             F = ring([jnp.concatenate([facing[n, p, 5 * t + f] for t in range(3)], axis=0) for p in range(3)])
-            M = [own_pack[f, p] for p in range(3)]
             F_own = [own_rows_of(v) for v in F]
             for p in range(2):
                 face_pad[f, p, 8:32, :] = F[p]
@@ -397,15 +400,13 @@
             azimuthal = [jnp.zeros((16, 128), F32)] * 2
             for d in range(-4, 5):
                 shifted = by_cells(F if d < 4 else F_own, d)
-                if d < 4:
-                    shifted_own = by_cells(M, d)
                 for p in range(2):
                     if d != 0:
                         weight = STENCIL[d - 1] if d > 0 else -STENCIL[-d - 1]
                         azimuthal[p] = azimuthal[p] + weight * (own_rows_of(shifted[p]) if d < 4 else shifted[p])
                     if d < 4:
                         ghost_own[p] = ghost_own[p] + coef_own[p][d + 4:d + 5, :] * shifted[p]
-                        ghost_face[p] = ghost_face[p] + coef_face[p][d + 4:d + 5, :] * shifted_own[p]
+                        ghost_face[p] = ghost_face[p] + coef_face[p][d + 4:d + 5, :] * own_shifted[f, d + 4, p]
             for p in range(2):
                 slope[1, f, p] = own_rows_of(radial_of(face_pad, f, p))
                 slope[2, f, p] = azimuthal[p]
@@ -497,7 +498,6 @@
             vmem(3, 2, 8, 128),
             vmem(3, 24, 128),
             vmem(3, 24, 128),
-            vmem(5, 3, 16, 128),
             vmem(5, 2, 40, 128),
             vmem(3, 5, 2, 16, 128),
             vmem(5, 2, 16, 128),
@@ -507,6 +507,7 @@
             vmem(5, 8, 16, 128),
             vmem(128, 128),
             vmem(128, 128),
+            vmem(5, 8, 2, 16, 128),
             pltpu.SemaphoreType.DMA((2, 40)),
             pltpu.SemaphoreType.DMA((2, 40)),
             pltpu.SemaphoreType.DMA((3,)),

time: 58.2 us -> 59 us (1.014)
  Pallas kernels: 56.3 us -> 57.1 us
    pallas_call x1, Pallas kernels: 56.3 us -> 57.1 us  [shards(): pl.pallas_call(kernel, out_shape=[jax.ShapeDtypeStruct(acoustic_state.sha...]
where the time goes in v7:
time: 59 us; the launch traced here: 58.9 us
  Pallas kernels  57.1 us (97%)
  other arithmetic  1.84 us (3%)
    pallas_call x1, Pallas kernels, shards(): pl.pallas_call(kernel, out_shape=[jax.ShapeDtypeStruct(acoustic_state.sha...  57.1 us
    add x1, other arithmetic, shards(): return without + ghosts  1.84 us

profile of v7, /device:TPU:1, one launch (start us, length us, event | category | flops | bytes accessed | tf_op | source)
XLA Modules:
  0.0 58.9 jit_solution(15878849615097403242)
XLA Ops:
  0.0 57.1 %acoustic_steps.1 = (f32[5,8,16,128]{3,2,1,0:T(8,128)}, f32[5,8,16,128]{3,2,1,0:T(8,128)}) custom-call(s32[2]{0:T(128)} %offset_hbm.1, s32[2,8]{1,0:T(2,128)} %shift_hbm.1, s32[2,8]{1,0:T(2,128)} %start_hbm.1, f32[2,8]{1,0:T(2,128)} %fraction_hbm.1, f32[3,16,128]{2,1,0:T(8,128)} %flow_hbm.1, f32[5,8,16,128]{3,2,1,0:T(8,128)} %state_hbm.1), custom_call_target="tpu_custom_call" | custom-call | tf_op jit(solution)/shard_map/acoustic_steps/pallas_call | solution.py:484
  57.1 1.8 %add.3 = f32[5,8,16,128]{3,2,1,0:T(8,128)} add(f32[5,8,16,128]{3,2,1,0:T(8,128)} %get-tuple-element.7, f32[5,8,16,128]{3,2,1,0:T(8,128)} %get-tuple-element.8) | non-fusion elementwise | flops 81920 | bytes 983040 | tf_op jit(solution)/shard_map/add | solution.py:520
